TPU v7x, 128 devices: a whole 4x4x4 slice. The times are simulated.
128 devices in a mesh: step: 2 (over core), tile: 64 (over z, y, x).
Axes of the slice: x: 4, y: 4, z: 4, core: 2. Of those that a mesh axis runs over, the one named last changes fastest.
Arguments:
- latents: float32 [2, 8192, 3072], P('step', 'tile'), may hold values from -6 to 6
- start: float32 [8192, 3072], P('tile'), may hold values from -6 to 6
- cached_velocity: float32 [2, 8192, 3072], P('step', 'tile'), may hold values from -4 to 4
- shift: float32 [2, 3072], P('step'), may hold values from -3 to 3
- scale: float32 [2, 3072], P('step'), may hold values from -3 to 3
- gate: float32 [2, 3072], P('step'), may hold values from -10 to 10
- step_sizes: float32 [2], P('step'), may hold values from 0.1 to 0.5
- converged: int32 [2, 64], P(None, 'tile'), may hold values from 0 to 1, as said below
- neighbours: int32 [64, 4], P('tile'), may hold values from 0 to 1, as said below
- w_qkv: bfloat16 [3, 3072, 2048], P(None, None, 'step'), may hold values from -0.109375 to 0.109375
- q_gain: float32 [128], replicated, may hold values from 0.1 to 1.9
- k_gain: float32 [128], replicated, may hold values from 0.1 to 1.9
- w_out: bfloat16 [2048, 3072], P('step', 'tile'), may hold values from -0.5 to 0.5
Outputs:
- updated: float32 [2, 8192, 3072], P('step', 'tile')
- velocity: float32 [2, 8192, 3072], P('step', 'tile')
Inputs may be any that keep to these rules, and one draw needn't show every extreme that they name: For each tile the converged steps are the first ones of the window, at most 1 of them. `neighbours`: an entry is 0 wherever the grid of 16 rows of 4 tiles has no neighbour that way.
All inputs are finite; a program needn't handle non-finite values.
Results may differ from a plain program's by a relative error of at most 0.008.
Values may be sent and summed in bfloat16 or wider, within the bound.
No kernel may reach another device: no remote copies, remote signals or barrier semaphores. Data moves between devices by JAX's collectives and lax.ppermute only.
A program may use at most 128 MiB of HBM per device.

v0:
```python
import jax
import jax.numpy as jnp
from jax import lax
from jax.experimental import pallas as pl
from jax.experimental.pallas import tpu as pltpu
from jax.sharding import PartitionSpec as P

GRID_COLS = 4
SIDE = 4
TILES = SIDE**3
F32 = jnp.float32
BF16 = jnp.bfloat16
NORM_COST = 16 * 10**9
OUTPUT_COST = 8 * 10**9
LOG2E = 1.4426950408889634
STRIDES = {"z": 16, "y": 4, "x": 1}
ORDERS = ((("x", "y", "z"), ("y", "x", "z")), (("x", "z", "y"), ("y", "z", "x")))
UNITS = (16, 32)
BOTH = ("step", "tile")
SWAP = [(0, 1), (1, 0)]


def partner(place, core, second):
    if core == second:
        return place ^ 1
    return (place + 1 if place % 2 else place - 1) % SIDE


def opposite(place, core, second):
    return (place + 2) % SIDE


def along(block, dims, second, target_of=partner):
    pairs = []
    for core in range(2):
        stride = STRIDES[dims[core]]
        for tile in range(TILES):
            place = tile // stride % SIDE
            target = tile + (target_of(place, core, second) - place) * stride
            pairs.append((core * TILES + tile, core * TILES + target))
    return lax.ppermute(block, BOTH, pairs)


def four(block, dims):
    first, second = along(block, dims, 0), along(block, dims, 1)
    return jnp.concatenate([block, first, second, along(block, dims, 0, opposite)], axis=0)


def neighbour_pairs(move):
    if abs(move) == 1:
        return [(t, t // GRID_COLS * GRID_COLS + (t + move) % GRID_COLS) for t in range(TILES)]
    return [(t, (t + move) % TILES) for t in range(TILES)]


def norm_kernel(x_any, scale_any, shift_any, out_ref, x_ref, scale_ref, shift_ref, sems):
    copies = [
        pltpu.make_async_copy(source, target, sems.at[i])
        for i, (source, target) in enumerate(((x_any, x_ref), (scale_any, scale_ref), (shift_any, shift_ref)))
    ]
    for copy in copies:
        copy.start()
    for copy in copies:
        copy.wait()
    x = x_ref[...]
    mean = jnp.mean(x, axis=-1, keepdims=True)
    centred = x - mean
    var = jnp.mean(centred * centred, axis=-1, keepdims=True)
    scaled = centred * (1.0 / jnp.sqrt(var + 1e-06)) * (1.0 + scale_ref[...]) + shift_ref[...]
    out_ref[...] = scaled.astype(BF16)


def limit(mib):
    return pltpu.CompilerParams(vmem_limit_bytes=mib << 20)


def normalize(x, scale, shift):
    rows, width = x.shape
    return pl.pallas_call(
        norm_kernel,
        in_specs=[pl.BlockSpec(memory_space=pltpu.HBM)] * 3,
        out_specs=pl.BlockSpec(memory_space=pltpu.VMEM),
        out_shape=jax.ShapeDtypeStruct((rows, width), BF16),
        scratch_shapes=[
            pltpu.VMEM((rows, width), F32),
            pltpu.VMEM((1, width), F32),
            pltpu.VMEM((1, width), F32),
            pltpu.SemaphoreType.DMA((3,)),
        ],
        compiler_params=limit(8),
        cost_estimate=pl.CostEstimate(flops=NORM_COST, transcendentals=0, bytes_accessed=6 * rows * width),
    )(*(pltpu.with_memory_space_constraint(value, pltpu.HBM) for value in (x, scale, shift)))


def make_project_kernel(head, first, parts, normed_parts, span):
    def kernel(own_ref, other_ref, w_ref, gain_ref, out_ref, x_ref):
        tokens = own_ref.shape[0]
        x_ref[:tokens, :] = own_ref[...]
        x_ref[tokens:, :] = other_ref[...]
        ones = jnp.full((head, head), 1.0 / head, BF16)
        for part in range(parts):
            for at in range(0, w_ref.shape[2], span):
                acc = jnp.dot(x_ref[...], w_ref[first + part, :, at : at + span], preferred_element_type=F32)
                if part < normed_parts:
                    blocks = []
                    for h in range(span // head):
                        block = acc[:, h * head : (h + 1) * head]
                        mean = jnp.dot((block * block).astype(BF16), ones, preferred_element_type=F32)
                        blocks.append((block * lax.rsqrt(mean + 1e-06) * gain_ref[...]).astype(BF16))
                    done = jnp.concatenate(blocks, axis=1)
                else:
                    done = acc.astype(BF16)
                out_ref[part, 0, :, at : at + span] = done[:tokens]
                out_ref[part, 1, :, at : at + span] = done[tokens:]

    return kernel


def project(own, other, w_qkv, gain, first, parts, normed_parts):
    tokens, width = own.shape
    cols = w_qkv.shape[2]
    return pl.pallas_call(
        make_project_kernel(gain.shape[-1], first, parts, normed_parts, cols // 2),
        in_specs=[pl.BlockSpec(memory_space=pltpu.VMEM)] * 4,
        out_specs=pl.BlockSpec(memory_space=pltpu.VMEM),
        out_shape=jax.ShapeDtypeStruct((parts, 2, tokens, cols), BF16),
        scratch_shapes=[pltpu.VMEM((2 * tokens, width), BF16)],
        compiler_params=limit(8),
        cost_estimate=pl.CostEstimate(
            flops=4 * tokens * width * cols * parts,
            transcendentals=0,
            bytes_accessed=2 * (parts * width * cols + 2 * tokens * width),
        ),
    )(own, other, w_qkv, gain)


def make_attend_kernel(head, factor):
    def kernel(near_ref, q_ref, own_ref, a_ref, b_ref, c_ref, d_ref, out_ref):
        sources = (own_ref, a_ref, b_ref, c_ref, d_ref)
        tokens = q_ref.shape[2]
        ones = jnp.ones((tokens, head), BF16)
        masks = [None] + [near_ref[0, j].astype(F32).astype(BF16) for j in range(4)]
        counts = jnp.concatenate([ones if mask is None else ones * mask for mask in masks], axis=0)
        for s in range(q_ref.shape[1]):
            for h in range(q_ref.shape[3] // head):
                lanes = slice(h * head, (h + 1) * head)
                keys = jnp.concatenate([ref[0, s, :, lanes] for ref in sources], axis=0)
                values = jnp.concatenate(
                    [
                        ref[1, s, :, lanes] if mask is None else ref[1, s, :, lanes] * mask
                        for ref, mask in zip(sources, masks)
                    ],
                    axis=0,
                )
                scores = lax.dot_general(
                    q_ref[0, s, :, lanes], keys, (((1,), (1,)), ((), ())), preferred_element_type=F32
                )
                p = jnp.exp2(scores * (factor * LOG2E)).astype(BF16)
                both = jnp.dot(p, jnp.concatenate([values, counts], axis=1), preferred_element_type=F32)
                out_ref[s, :, lanes] = (both[:, :head] / both[:, head:]).astype(BF16)

    return kernel


def attention(near, queries, sources, head):
    _, steps, tokens, cols = queries.shape
    factor = 1.0 / float(head) ** 0.5
    return pl.pallas_call(
        make_attend_kernel(head, factor),
        in_specs=[pl.BlockSpec(memory_space=pltpu.SMEM)]
        + [pl.BlockSpec(memory_space=pltpu.VMEM)] * (1 + len(sources)),
        out_specs=pl.BlockSpec(memory_space=pltpu.VMEM),
        out_shape=jax.ShapeDtypeStruct((steps, tokens, cols), BF16),
        compiler_params=limit(8),
        cost_estimate=pl.CostEstimate(
            flops=4 * steps * tokens * 5 * tokens * cols,
            transcendentals=steps * tokens * 5 * tokens * cols // head,
            bytes_accessed=2 * 12 * steps * tokens * cols,
        ),
    )(near, queries, *sources)


def slot_place(place, core, slot):
    if slot == 0:
        return place
    if slot == 3:
        return place ^ 2
    near = place ^ 1
    far = (place + 2 * (place & 1) - 1) & (SIDE - 1)
    return jnp.where(core == slot - 1, near, far)


def make_output_kernel(shard):
    def kernel(place_ref, a_ref, *refs):
        pieces, out_ref, w_ref, sem = refs[:-3], refs[-3], refs[-2], refs[-1]
        core = place_ref[0]
        where = {"z": 1, "y": 2, "x": 3}
        for colour, orders in enumerate(ORDERS):
            unit = UNITS[colour]
            parts = []
            for level in range(3):
                first, second = orders[0][level], orders[1][level]
                place = jnp.where(core == 0, place_ref[where[first]], place_ref[where[second]])
                stride = jnp.where(core == 0, STRIDES[first], STRIDES[second])
                parts.append([slot_place(place, core, slot) * stride for slot in range(SIDE)])
            mine = pieces[:SIDE] if colour == 0 else pieces[SIDE:]
            blocks = [[(ref, at * unit) for at in range(SIDE * SIDE)] for ref in mine[: SIDE - 1]]
            count = SIDE * SIDE // len(mine[SIDE - 1 :])
            blocks.append([(ref, at * unit) for ref in mine[SIDE - 1 :] for at in range(count)])
            for slot in range(SIDE):
                for at, (ref, row) in enumerate(blocks[slot]):
                    tile = parts[2][slot] + parts[1][at // SIDE] + parts[0][at % SIDE]
                    target = pl.multiple_of(tile * shard + sum(UNITS[:colour]), 8)
                    pltpu.make_async_copy(ref.at[pl.ds(row, unit)], w_ref.at[pl.ds(target, unit)], sem).start()
        pltpu.make_async_copy(w_ref, w_ref, sem).wait()
        steps, tokens, cols = a_ref.shape
        left = a_ref[...].reshape(steps * tokens, cols)
        chunk = 512
        for at in range(0, w_ref.shape[0], chunk):
            right = w_ref[at : at + chunk, :]
            done = lax.dot_general(left, right, (((1,), (1,)), ((), ())), preferred_element_type=F32).astype(BF16)
            for s in range(steps):
                out_ref[1 - s, :, at : at + chunk] = done[s * tokens : (s + 1) * tokens]

    return kernel


def output_project(place, attended, pieces, width, shard):
    steps, tokens, cols = attended.shape
    return pl.pallas_call(
        make_output_kernel(shard),
        in_specs=[
            pl.BlockSpec(memory_space=pltpu.SMEM),
            pl.BlockSpec(memory_space=pltpu.VMEM),
        ]
        + [pl.BlockSpec(memory_space=pltpu.HBM)] * len(pieces),
        out_specs=pl.BlockSpec(memory_space=pltpu.VMEM),
        out_shape=jax.ShapeDtypeStruct((steps, tokens, width), BF16),
        scratch_shapes=[pltpu.VMEM((width, cols), BF16), pltpu.SemaphoreType.DMA],
        compiler_params=limit(16),
        cost_estimate=pl.CostEstimate(
            flops=OUTPUT_COST,
            transcendentals=0,
            bytes_accessed=2 * (cols * width + steps * tokens * (cols + width)),
        ),
    )(place, attended, *(pltpu.with_memory_space_constraint(piece, pltpu.HBM) for piece in pieces))


def make_finish_kernel(parts):
    def kernel(
        place_ref, converged_ref, terms_ref, arrived_ref, start_ref, cached_ref, gate_ref, held_ref, pace_ref,
        updated_ref, velocity_ref, buf_ref, sems,
    ):
        frozen = converged_ref[place_ref[0]] > 0
        frozen_first = converged_ref[0] > 0
        gate = gate_ref[...]
        pace = pace_ref[...]
        rows = buf_ref.shape[2]
        copies = []
        for i in range(parts):
            at = slice(i * rows, (i + 1) * rows)
            mine = terms_ref[1, at, :].astype(F32) + arrived_ref[0, at, :].astype(F32)
            buf_ref[i, 1] = jnp.where(frozen, cached_ref[at, :], gate * mine)
            theirs = terms_ref[0, at, :].astype(F32) + arrived_ref[1, at, :].astype(F32)
            prefix = jnp.where(frozen_first, held_ref[at, :].astype(F32), pace * theirs)
            buf_ref[i, 0] = start_ref[at, :] + prefix
            for j, ref in enumerate((updated_ref, velocity_ref)):
                copy = pltpu.make_async_copy(buf_ref.at[i, j], ref.at[pl.ds(i * rows, rows)], sems.at[i, j])
                copy.start()
                copies.append(copy)
        for copy in copies:
            copy.wait()

    return kernel


def finish(place, converged, terms, arrived, start, cached, gate, held, pace):
    tokens, width = start.shape
    parts = 4
    out = jax.ShapeDtypeStruct((tokens, width), F32)
    return pl.pallas_call(
        make_finish_kernel(parts),
        in_specs=[pl.BlockSpec(memory_space=pltpu.SMEM)] * 2 + [pl.BlockSpec(memory_space=pltpu.VMEM)] * 7,
        out_specs=[pl.BlockSpec(memory_space=pltpu.HBM)] * 2,
        out_shape=[out, out],
        scratch_shapes=[
            pltpu.VMEM((parts, 2, tokens // parts, width), F32),
            pltpu.SemaphoreType.DMA((parts, 2)),
        ],
        compiler_params=limit(8),
        cost_estimate=pl.CostEstimate(
            flops=8 * tokens * width, transcendentals=0, bytes_accessed=26 * tokens * width
        ),
    )(place, converged, terms, arrived, start, cached, gate, held, pace)


def start_gather(w_out):
    dims = tuple(order[0] for order in ORDERS[0])
    block = w_out.T[None]
    block = four(block, dims)
    parts, at = [], 0
    for unit in UNITS:
        parts.append(block[:, at : at + unit].reshape(SIDE * unit, -1))
        at += unit
    return parts


def finish_gather(colour, line):
    orders = ORDERS["ab".index(colour)]
    dims = tuple(order[1] for order in orders)
    plane = four(line, dims)
    dims = tuple(order[2] for order in orders)
    first, second = along(plane, dims, 0), along(plane, dims, 1)
    if colour == "a":
        return [plane, first, second, along(first, dims, 1)]
    half = plane.shape[0] // 2
    low = along(first[:half], dims, 1)
    return [plane, first, second, low, along(second[half:], dims, 0)]


def body(
    latents,
    start,
    cached_velocity,
    shift,
    scale,
    gate,
    step_sizes,
    converged,
    neighbours,
    w_qkv,
    q_gain,
    k_gain,
    w_out,
):
    _, width = latents.shape[1:]
    head = q_gain.shape[0]
    shard = w_out.shape[1]
    here = lax.axis_index("step")
    tile = lax.axis_index("tile")
    place = jnp.stack([here, tile // 16, tile // 4 % 4, tile % 4]).astype(jnp.int32)

    own = normalize(latents[0], scale, shift)
    other = lax.ppermute(own, "step", SWAP)

    lines = start_gather(w_out)
    pieces = finish_gather("a", lines[0]) + finish_gather("b", lines[1])

    pair = project(own, other, w_qkv, k_gain[None], 1, 2, 1)
    around = []
    for move in (1, -1, GRID_COLS, -GRID_COLS):
        around.append(lax.ppermute(pair, "tile", neighbour_pairs(move)))
    step_size = step_sizes[0]
    to_send = (step_size * cached_velocity[0]).astype(BF16)
    sent_cached = lax.ppermute(to_send, "step", [(0, 1)])
    sent_gate = lax.ppermute(step_size * gate, "step", [(0, 1)])
    queries = project(own, other, w_qkv, q_gain[None], 0, 1, 1)
    queries, sent_cached, sent_gate = lax.optimization_barrier((queries, sent_cached, sent_gate))
    attended = attention(neighbours, queries, [pair] + around, head)
    terms = output_project(place, attended, pieces, width, shard)

    arrived = lax.ppermute(terms, "step", SWAP)
    updated, velocity = finish(
        place, converged[:, 0], terms, arrived, start, cached_velocity[0], gate, sent_cached, sent_gate
    )
    return (updated[None], velocity[None])


def solution(mesh):
    placed = (
        P("step", "tile", None),
        P("tile", None),
        P("step", "tile", None),
        P("step", None),
        P("step", None),
        P("step", None),
        P("step"),
        P(None, "tile"),
        P("tile", None),
        P(None, None, "step"),
        P(),
        P(),
        P("step", "tile"),
    )

    return jax.shard_map(
        body,
        mesh=mesh,
        in_specs=placed,
        out_specs=(P("step", "tile", None), P("step", "tile", None)),
        check_vma=False,
    )
```

profile of v0, /device:TPU:1, one launch (start us, length us, event | category | flops | bytes accessed | tf_op | source)
XLA Modules:
  0.0 102.5 jit_solution(17083973406585283111)
XLA Ops:
  0.6 3.8 %collective-permute-start.9 = (bf16[1,48,1024]{2,1,0:T(8,128)(2,1)}, bf16[1,48,1024]{2,1,0:T(8,128)(2,1)S(1)}, u32[]{:S(2)}, u32[]{:S(2)}) collective-permute-start(bf16[1,48,1024]{2,1,0:T(8,128)(2,1)} %bitcast.34), channel_id=1, source_target_pairs={{0,2},{1,3},{2,0},{3,1},{4,6},{5,7},{6,4},{7,5},{8,10},{9,11},{10,... | collective-permute-start | bytes 294920 | tf_op jit(solution)/shard_map/ppermute | solution.py:41
  5.2 1.4 %collective-permute-done.9 = bf16[1,48,1024]{2,1,0:T(8,128)(2,1)S(1)} collective-permute-done((bf16[1,48,1024]{2,1,0:T(8,128)(2,1)}, bf16[1,48,1024]{2,1,0:T(8,128)(2,1)S(1)}, u32[]{:S(2)}, u32[]{:S(2)}) %collective-permute-start.9) | collective-permute-done | bytes 98336 | tf_op jit(solution)/shard_map/ppermute | solution.py:41
  6.7 1.5 %collective-permute-done.8 = bf16[1,48,1024]{2,1,0:T(8,128)(2,1)S(1)} collective-permute-done((bf16[1,48,1024]{2,1,0:T(8,128)(2,1)}, bf16[1,48,1024]{2,1,0:T(8,128)(2,1)S(1)}, u32[]{:S(2)}, u32[]{:S(2)}) %collective-permute-start.8) | collective-permute-done | bytes 98336 | tf_op jit(solution)/shard_map/ppermute | solution.py:41
  8.1 1.9 %collective-permute-done.7 = bf16[1,48,1024]{2,1,0:T(8,128)(2,1)S(1)} collective-permute-done((bf16[1,48,1024]{2,1,0:T(8,128)(2,1)}, bf16[1,48,1024]{2,1,0:T(8,128)(2,1)S(1)}, u32[]{:S(2)}, u32[]{:S(2)}) %collective-permute-start.7) | collective-permute-done | bytes 98336 | tf_op jit(solution)/shard_map/ppermute | solution.py:41
  10.8 2.5 %collective-permute-start.12 = (bf16[64,1024]{1,0:T(8,128)(2,1)S(1)}, bf16[64,1024]{1,0:T(8,128)(2,1)S(1)}, u32[]{:S(2)}, u32[]{:S(2)}) collective-permute-start(bf16[64,1024]{1,0:T(8,128)(2,1)S(1)} %bitcast.30), channel_id=1, source_target_pairs={{0,8},{1,9},{2,10},{3,11},{4,12},{5,13},{6,14},{7,15},{8,0},{9,1},... | collective-permute-start | bytes 393224 | tf_op jit(solution)/shard_map/ppermute | solution.py:41
  15.0 3.7 %collective-permute-start.18 = (bf16[128,1024]{1,0:T(8,128)(2,1)S(1)}, bf16[128,1024]{1,0:T(8,128)(2,1)S(1)}, u32[]{:S(2)}, u32[]{:S(2)}) collective-permute-start(bf16[128,1024]{1,0:T(8,128)(2,1)S(1)} %bitcast.26), channel_id=1, source_target_pairs={{0,32},{1,33},{2,34},{3,35},{4,36},{5,37},{6,38},{7,39},{8,40},{9,... | collective-permute-start | bytes 786440 | tf_op jit(solution)/shard_map/ppermute | solution.py:41
  20.0 2.1 %shard_map.140.own_ref = bf16[128,3072]{1,0:T(8,128)(2,1)S(1)} custom-call(f32[128,3072]{1,0:T(8,128)} %bitcast.39, f32[1,3072]{1,0:T(1,128)} %scale_any.1, f32[1,3072]{1,0:T(1,128)} %shift_any.1), custom_call_target="tpu_custom_call" | custom-call | flops 16000000000 | bytes 2359296 | tf_op jit(solution)/shard_map/pallas_call | solution.py:78
  23.6 2.3 %collective-permute-start = (bf16[128,3072]{1,0:T(8,128)(2,1)S(1)}, bf16[128,3072]{1,0:T(8,128)(2,1)S(1)}, u32[]{:S(2)}, u32[]{:S(2)}) collective-permute-start(bf16[128,3072]{1,0:T(8,128)(2,1)S(1)} %shard_map.140.own_ref), channel_id=1, source_target_pairs={{0,64},{64,0},{1,65},{65,1},{2,66},{66,2},{3,67},{67,3},{4,68},{68... | collective-permute-start | bytes 2359304 | tf_op jit(solution)/shard_map/ppermute | solution.py:343
  26.7 2.3 %collective-permute-start.13 = (bf16[256,1024]{1,0:T(8,128)(2,1)}, bf16[256,1024]{1,0:T(8,128)(2,1)}, u32[]{:S(2)}, u32[]{:S(2)}) collective-permute-start(bf16[256,1024]{1,0:T(8,128)(2,1)} %pad_maximum_fusion.1.refs_0_), channel_id=1, source_target_pairs={{0,16},{1,17},{2,18},{3,19},{4,20},{5,21},{6,22},{7,23},{8,24},{9,... | collective-permute-start | bytes 1572872 | tf_op jit(solution)/shard_map/ppermute | solution.py:41
  29.4 1.5 %collective-permute-done.16 = bf16[128,1024]{1,0:T(8,128)(2,1)S(1)} collective-permute-done((bf16[128,1024]{1,0:T(8,128)(2,1)S(1)}, bf16[128,1024]{1,0:T(8,128)(2,1)S(1)}, u32[]{:S(2)}, u32[]{:S(2)}) %collective-permute-start.16) | collective-permute-done | bytes 262176 | tf_op jit(solution)/shard_map/ppermute | solution.py:41
  30.9 2.2 %collective-permute-start.19 = (bf16[512,1024]{1,0:T(8,128)(2,1)S(1)}, bf16[512,1024]{1,0:T(8,128)(2,1)S(1)}, u32[]{:S(2)}, u32[]{:S(2)}) collective-permute-start(bf16[512,1024]{1,0:T(8,128)(2,1)S(1)} %pad_maximum_fusion.refs_4_), channel_id=1, source_target_pairs={{0,4},{1,5},{2,6},{3,7},{4,0},{5,1},{6,2},{7,3},{8,12},{9,13},{10,... | collective-permute-start | bytes 3145736 | tf_op jit(solution)/shard_map/ppermute | solution.py:41
  33.1 1.3 %collective-permute-start.2 = (f32[1,3072]{1,0:T(1,128)S(1)}, f32[1,3072]{1,0:T(1,128)S(1)}, u32[]{:S(2)}, u32[]{:S(2)}) collective-permute-start(f32[1,3072]{1,0:T(1,128)S(1)} %broadcast_multiply_fusion), channel_id=1, source_target_pairs={{0,64},{1,65},{2,66},{3,67},{4,68},{5,69},{6,70},{7,71},{8,72},{9,... | collective-permute-start | bytes 36872 | tf_op jit(solution)/shard_map/ppermute | solution.py:355
  34.8 3.8 %shard_map.142.own_ref = bf16[2,2,128,1024]{3,2,1,0:T(8,128)(2,1)S(1)} custom-call(bf16[128,3072]{1,0:T(8,128)(2,1)S(1)} %shard_map.140.own_ref, bf16[128,3072]{1,0:T(8,128)(2,1)S(1)} %collective-permute-done.other_ref, bf16[3,3072,1024]{2,1,0:T(8,128)(2,1)S(1)} %bitcast.21, f32[1,128]{1,0:T(1,128)S(1)} %bitcast.23), custom_call_target="tpu_custom_call" | custom-call | flops 3221225472 | bytes 14155776 | tf_op jit(solution)/shard_map/pallas_call | solution.py:121
  38.7 1.3 %collective-permute-start.3 = (bf16[2,2,128,1024]{3,2,1,0:T(8,128)(2,1)S(1)}, bf16[2,2,128,1024]{3,2,1,0:T(8,128)(2,1)S(1)}, u32[]{:S(2)}, u32[]{:S(2)}) collective-permute-start(bf16[2,2,128,1024]{3,2,1,0:T(8,128)(2,1)S(1)} %shard_map.142.own_ref), channel_id=1, source_target_pairs={{0,1},{1,2},{2,3},{3,0},{4,5},{5,6},{6,7},{7,4},{8,9},{9,10},{10,1... | collective-permute-start | bytes 3145736 | tf_op jit(solution)/shard_map/ppermute | solution.py:351
  40.0 1.4 %collective-permute-start.4 = (bf16[2,2,128,1024]{3,2,1,0:T(8,128)(2,1)S(1)}, bf16[2,2,128,1024]{3,2,1,0:T(8,128)(2,1)S(1)}, u32[]{:S(2)}, u32[]{:S(2)}) collective-permute-start(bf16[2,2,128,1024]{3,2,1,0:T(8,128)(2,1)S(1)} %shard_map.142.own_ref), channel_id=1, source_target_pairs={{0,3},{1,0},{2,1},{3,2},{4,7},{5,4},{6,5},{7,6},{8,11},{9,8},{10,9... | collective-permute-start | bytes 3145736 | tf_op jit(solution)/shard_map/ppermute | solution.py:351
  41.6 5.8 %collective-permute-done.19.refs_5_ = bf16[512,1024]{1,0:T(8,128)(2,1)S(1)} collective-permute-done((bf16[512,1024]{1,0:T(8,128)(2,1)S(1)}, bf16[512,1024]{1,0:T(8,128)(2,1)S(1)}, u32[]{:S(2)}, u32[]{:S(2)}) %collective-permute-start.19) | collective-permute-done | bytes 1048608 | tf_op jit(solution)/shard_map/ppermute | solution.py:41
  47.3 1.3 %collective-permute-start.1 = (bf16[128,3072]{1,0:T(8,128)(2,1)S(1)}, bf16[128,3072]{1,0:T(8,128)(2,1)S(1)}, u32[]{:S(2)}, u32[]{:S(2)}) collective-permute-start(bf16[128,3072]{1,0:T(8,128)(2,1)S(1)} %multiply_convert_fusion), channel_id=1, source_target_pairs={{0,64},{1,65},{2,66},{3,67},{4,68},{5,69},{6,70},{7,71},{8,72},{9,... | collective-permute-start | bytes 2359304 | tf_op jit(solution)/shard_map/ppermute | solution.py:354
  48.6 4.0 %collective-permute-done.20.refs_6_ = bf16[512,1024]{1,0:T(8,128)(2,1)S(1)} collective-permute-done((bf16[512,1024]{1,0:T(8,128)(2,1)S(1)}, bf16[512,1024]{1,0:T(8,128)(2,1)S(1)}, u32[]{:S(2)}, u32[]{:S(2)}) %collective-permute-start.20) | collective-permute-done | bytes 1048608 | tf_op jit(solution)/shard_map/ppermute | solution.py:41
  52.6 2.8 %collective-permute-start.6 = (bf16[2,2,128,1024]{3,2,1,0:T(8,128)(2,1)S(1)}, bf16[2,2,128,1024]{3,2,1,0:T(8,128)(2,1)}, u32[]{:S(2)}, u32[]{:S(2)}) collective-permute-start(bf16[2,2,128,1024]{3,2,1,0:T(8,128)(2,1)S(1)} %shard_map.142.own_ref), channel_id=1, source_target_pairs={{0,60},{1,61},{2,62},{3,63},{4,0},{5,1},{6,2},{7,3},{8,4},{9,5},{1... | collective-permute-start | bytes 3145736 | tf_op jit(solution)/shard_map/ppermute | solution.py:351
  57.9 11.0 %collective-permute-done.3.a_ref = bf16[2,2,128,1024]{3,2,1,0:T(8,128)(2,1)S(1)} collective-permute-done((bf16[2,2,128,1024]{3,2,1,0:T(8,128)(2,1)S(1)}, bf16[2,2,128,1024]{3,2,1,0:T(8,128)(2,1)S(1)}, u32[]{:S(2)}, u32[]{:S(2)}) %collective-permute-start.3) | collective-permute-done | bytes 1048608 | tf_op jit(solution)/shard_map/ppermute | solution.py:351
  69.9 1.0 collective-permute-start.15
  71.0 1.0 copy-done.7
  72.0 2.2 %collective-permute-start.21 = (bf16[256,1024]{1,0:T(8,128)(2,1)}, bf16[256,1024]{1,0:T(8,128)(2,1)}, u32[]{:S(2)}, u32[]{:S(2)}) collective-permute-start(bf16[256,1024]{1,0:T(8,128)(2,1)} %slice.16), channel_id=1, source_target_pairs={{0,12},{1,13},{2,14},{3,15},{4,8},{5,9},{6,10},{7,11},{8,4},{9,5},... | collective-permute-start | bytes 1572872 | tf_op jit(solution)/shard_map/ppermute | solution.py:41
  74.2 1.0 copy-done.9
  75.4 6.4 %copy-done = bf16[3,3072,1024]{2,1,0:T(8,128)(2,1)S(1)} copy-done((bf16[3,3072,1024]{2,1,0:T(8,128)(2,1)S(1)}, bf16[3,3072,1024]{2,1,0:T(8,128)(2,1)}, u32[]{:S(2)}) %copy-start) | copy-done | bytes 18874392
  81.8 1.1 %copy-done.3 = bf16[128,3072]{1,0:T(8,128)(2,1)S(1)} copy-done((bf16[128,3072]{1,0:T(8,128)(2,1)S(1)}, bf16[128,3072]{1,0:T(8,128)(2,1)}, u32[]{:S(2)}) %copy-start.3) | copy-done | bytes 786456
  82.9 2.1 %shard_map.141.q_ref = bf16[1,2,128,1024]{3,2,1,0:T(8,128)(2,1)S(1)} custom-call(bf16[128,3072]{1,0:T(8,128)(2,1)S(1)} %shard_map.140.own_ref, bf16[128,3072]{1,0:T(8,128)(2,1)S(1)} %copy-done.3, bf16[3,3072,1024]{2,1,0:T(8,128)(2,1)S(1)} %copy-done, f32[1,128]{1,0:T(1,128)S(1)} %bitcast.24), custom_call_target="tpu_custom_call" | custom-call | flops 1610612736 | bytes 7864320 | tf_op jit(solution)/shard_map/pallas_call | solution.py:121
  85.1 3.2 %shard_map.143.a_ref = bf16[2,128,1024]{2,1,0:T(8,128)(2,1)S(1)} custom-call(s32[1,4]{1,0:T(1,128)S(1)} %copy-done.16, bf16[1,2,128,1024]{3,2,1,0:T(8,128)(2,1)S(1)} %shard_map.141.q_ref, bf16[2,2,128,1024]{3,2,1,0:T(8,128)(2,1)S(1)} %shard_map.142.own_ref, bf16[2,2,128,1024]{3,2,1,0:T(8,128)(2,1)S(1)} %copy-done.6, bf16[2,2,128,1024]{3,2,1,0:T(8,128)(2,1)S(1)} %copy-done.8, ...), custom_call_target="tpu_custom_call" | custom-call | flops 671088640 | bytes 6291456 | tf_op jit(solution)/shard_map/pallas_call | solution.py:167
  88.4 5.3 %shard_map.144.terms_ref = bf16[2,128,3072]{2,1,0:T(8,128)(2,1)S(1)} custom-call(s32[4]{0:T(128)S(1)} %pad_add_fusion.place_ref, bf16[2,128,1024]{2,1,0:T(8,128)(2,1)S(1)} %shard_map.143.a_ref, bf16[256,1024]{1,0:T(8,128)(2,1)} %pad_maximum_fusion.1.refs_0_, bf16[256,1024]{1,0:T(8,128)(2,1)} %collective-permute-done.13.refs_1_, ...), custom_call_target="tpu_custom_call" | custom-call | flops 8000000000 | bytes 8388608 | tf_op jit(solution)/shard_map/pallas_call | solution.py:229
  93.8 3.1 %collective-permute-start.23 = (bf16[2,128,3072]{2,1,0:T(8,128)(2,1)S(1)}, bf16[2,128,3072]{2,1,0:T(8,128)(2,1)S(1)}, u32[]{:S(2)}, u32[]{:S(2)}) collective-permute-start(bf16[2,128,3072]{2,1,0:T(8,128)(2,1)S(1)} %shard_map.144.terms_ref), channel_id=1, source_target_pairs={{0,64},{64,0},{1,65},{65,1},{2,66},{66,2},{3,67},{67,3},{4,68},{68... | collective-permute-start | bytes 4718600 | tf_op jit(solution)/shard_map/ppermute | solution.py:361
  96.8 3.0 %collective-permute-done.23.arrived_ref = bf16[2,128,3072]{2,1,0:T(8,128)(2,1)S(1)} collective-permute-done((bf16[2,128,3072]{2,1,0:T(8,128)(2,1)S(1)}, bf16[2,128,3072]{2,1,0:T(8,128)(2,1)S(1)}, u32[]{:S(2)}, u32[]{:S(2)}) %collective-permute-start.23) | collective-permute-done | bytes 1572896 | tf_op jit(solution)/shard_map/ppermute | solution.py:361
  99.9 2.4 %shard_map.145 = (f32[128,3072]{1,0:T(8,128)}, f32[128,3072]{1,0:T(8,128)}) custom-call(s32[4]{0:T(128)S(1)} %pad_add_fusion.place_ref, s32[2]{0:T(128)S(1)} %bitcast.25, bf16[2,128,3072]{2,1,0:T(8,128)(2,1)S(1)} %shard_map.144.terms_ref, bf16[2,128,3072]{2,1,0:T(8,128)(2,1)S(1)} %collective-permute-done.23.arrived_ref, f32[128,3072]{1,0:T(8,128)S(1)} %copy-done.4, ...), custom_call_target="tpu_custom_call" | custom-call | flops 3145728 | bytes 10223616 | tf_op jit(solution)/shard_map/pallas_call | solution.py:280
  (84 shorter events, 10.1 us)
Async XLA Ops:
  0.6 6.0 %collective-permute-start.9 = (bf16[1,48,1024]{2,1,0:T(8,128)(2,1)}, bf16[1,48,1024]{2,1,0:T(8,128)(2,1)S(1)}, u32[]{:S(2)}, u32[]{:S(2)}) collective-permute-start(bf16[1,48,1024]{2,1,0:T(8,128)(2,1)} %bitcast.34), channel_id=1, source_target_pairs={{0,2},{1,3},{2,0},{3,1},{4,6},{5,7},{6,4},{7,5},{8,10},{9,11},{10,... | collective-permute-start | bytes 294920 | tf_op jit(solution)/shard_map/ppermute | solution.py:41
  4.4 3.7 %collective-permute-start.8 = (bf16[1,48,1024]{2,1,0:T(8,128)(2,1)}, bf16[1,48,1024]{2,1,0:T(8,128)(2,1)S(1)}, u32[]{:S(2)}, u32[]{:S(2)}) collective-permute-start(bf16[1,48,1024]{2,1,0:T(8,128)(2,1)} %bitcast.35), channel_id=1, source_target_pairs={{0,3},{1,2},{2,1},{3,0},{4,7},{5,6},{6,5},{7,4},{8,11},{9,10},{10,... | collective-permute-start | bytes 294920 | tf_op jit(solution)/shard_map/ppermute | solution.py:41
  4.8 5.2 %collective-permute-start.7 = (bf16[1,48,1024]{2,1,0:T(8,128)(2,1)}, bf16[1,48,1024]{2,1,0:T(8,128)(2,1)S(1)}, u32[]{:S(2)}, u32[]{:S(2)}) collective-permute-start(bf16[1,48,1024]{2,1,0:T(8,128)(2,1)} %bitcast.36), channel_id=1, source_target_pairs={{0,1},{1,0},{2,3},{3,2},{4,5},{5,4},{6,7},{7,6},{8,9},{9,8},{10,11... | collective-permute-start | bytes 294920 | tf_op jit(solution)/shard_map/ppermute | solution.py:41
  10.8 8.7 %collective-permute-start.12 = (bf16[64,1024]{1,0:T(8,128)(2,1)S(1)}, bf16[64,1024]{1,0:T(8,128)(2,1)S(1)}, u32[]{:S(2)}, u32[]{:S(2)}) collective-permute-start(bf16[64,1024]{1,0:T(8,128)(2,1)S(1)} %bitcast.30), channel_id=1, source_target_pairs={{0,8},{1,9},{2,10},{3,11},{4,12},{5,13},{6,14},{7,15},{8,0},{9,1},... | collective-permute-start | bytes 393224 | tf_op jit(solution)/shard_map/ppermute | solution.py:41
  13.3 10.2 %collective-permute-start.11 = (bf16[64,1024]{1,0:T(8,128)(2,1)S(1)}, bf16[64,1024]{1,0:T(8,128)(2,1)S(1)}, u32[]{:S(2)}, u32[]{:S(2)}) collective-permute-start(bf16[64,1024]{1,0:T(8,128)(2,1)S(1)} %bitcast.31), channel_id=1, source_target_pairs={{0,12},{1,13},{2,14},{3,15},{4,8},{5,9},{6,10},{7,11},{8,4},{9,5},... | collective-permute-start | bytes 393224 | tf_op jit(solution)/shard_map/ppermute | solution.py:41
  13.6 12.3 %collective-permute-start.10 = (bf16[64,1024]{1,0:T(8,128)(2,1)S(1)}, bf16[64,1024]{1,0:T(8,128)(2,1)S(1)}, u32[]{:S(2)}, u32[]{:S(2)}) collective-permute-start(bf16[64,1024]{1,0:T(8,128)(2,1)S(1)} %bitcast.32), channel_id=1, source_target_pairs={{0,4},{1,5},{2,6},{3,7},{4,0},{5,1},{6,2},{7,3},{8,12},{9,13},{10,... | collective-permute-start | bytes 393224 | tf_op jit(solution)/shard_map/ppermute | solution.py:41
  15.0 14.0 %collective-permute-start.18 = (bf16[128,1024]{1,0:T(8,128)(2,1)S(1)}, bf16[128,1024]{1,0:T(8,128)(2,1)S(1)}, u32[]{:S(2)}, u32[]{:S(2)}) collective-permute-start(bf16[128,1024]{1,0:T(8,128)(2,1)S(1)} %bitcast.26), channel_id=1, source_target_pairs={{0,32},{1,33},{2,34},{3,35},{4,36},{5,37},{6,38},{7,39},{8,40},{9,... | collective-permute-start | bytes 786440 | tf_op jit(solution)/shard_map/ppermute | solution.py:41
  18.7 10.6 %collective-permute-start.17 = (bf16[128,1024]{1,0:T(8,128)(2,1)S(1)}, bf16[128,1024]{1,0:T(8,128)(2,1)S(1)}, u32[]{:S(2)}, u32[]{:S(2)}) collective-permute-start(bf16[128,1024]{1,0:T(8,128)(2,1)S(1)} %bitcast.27), channel_id=1, source_target_pairs={{0,48},{1,49},{2,50},{3,51},{4,52},{5,53},{6,54},{7,55},{8,56},{9,... | collective-permute-start | bytes 786440 | tf_op jit(solution)/shard_map/ppermute | solution.py:41
  19.5 11.4 %collective-permute-start.16 = (bf16[128,1024]{1,0:T(8,128)(2,1)S(1)}, bf16[128,1024]{1,0:T(8,128)(2,1)S(1)}, u32[]{:S(2)}, u32[]{:S(2)}) collective-permute-start(bf16[128,1024]{1,0:T(8,128)(2,1)S(1)} %bitcast.28), channel_id=1, source_target_pairs={{0,16},{1,17},{2,18},{3,19},{4,20},{5,21},{6,22},{7,23},{8,24},{9,... | collective-permute-start | bytes 786440 | tf_op jit(solution)/shard_map/ppermute | solution.py:41
  20.0 14.8 %slice-start = ((s8[18874368]{0:T(1024)(128)(4,1)}), s8[4194304]{0:T(1024)(128)(4,1)S(1)}, s32[]{:S(2)}) async-start(s8[18874368]{0:T(1024)(128)(4,1)} %bitcast.20), calls=%async_computation | async-start | bytes 8388608
  20.0 14.8 %slice-start.1 = ((s8[18874368]{0:T(1024)(128)(4,1)}), s8[4194304]{0:T(1024)(128)(4,1)S(1)}, s32[]{:S(2)}) async-start(s8[18874368]{0:T(1024)(128)(4,1)} %bitcast.20), calls=%async_computation.1 | async-start | bytes 8388608
  20.0 14.8 %slice-start.2 = ((s8[18874368]{0:T(1024)(128)(4,1)}), s8[4194304]{0:T(1024)(128)(4,1)S(1)}, s32[]{:S(2)}) async-start(s8[18874368]{0:T(1024)(128)(4,1)} %bitcast.20), calls=%async_computation.2 | async-start | bytes 8388608
  20.0 14.8 %slice-start.3 = ((s8[18874368]{0:T(1024)(128)(4,1)}), s8[4194304]{0:T(1024)(128)(4,1)S(1)}, s32[]{:S(2)}) async-start(s8[18874368]{0:T(1024)(128)(4,1)} %bitcast.20), calls=%async_computation.3 | async-start | bytes 8388608
  20.0 14.8 %slice-start.4 = ((s8[18874368]{0:T(1024)(128)(4,1)}), s8[2097152]{0:T(1024)(128)(4,1)S(1)}, s32[]{:S(2)}) async-start(s8[18874368]{0:T(1024)(128)(4,1)} %bitcast.20), calls=%async_computation.4 | async-start | bytes 4194304
  23.6 11.2 %collective-permute-start = (bf16[128,3072]{1,0:T(8,128)(2,1)S(1)}, bf16[128,3072]{1,0:T(8,128)(2,1)S(1)}, u32[]{:S(2)}, u32[]{:S(2)}) collective-permute-start(bf16[128,3072]{1,0:T(8,128)(2,1)S(1)} %shard_map.140.own_ref), channel_id=1, source_target_pairs={{0,64},{64,0},{1,65},{65,1},{2,66},{66,2},{3,67},{67,3},{4,68},{68... | collective-permute-start | bytes 2359304 | tf_op jit(solution)/shard_map/ppermute | solution.py:343
  26.7 14.7 %collective-permute-start.13 = (bf16[256,1024]{1,0:T(8,128)(2,1)}, bf16[256,1024]{1,0:T(8,128)(2,1)}, u32[]{:S(2)}, u32[]{:S(2)}) collective-permute-start(bf16[256,1024]{1,0:T(8,128)(2,1)} %pad_maximum_fusion.1.refs_0_), channel_id=1, source_target_pairs={{0,16},{1,17},{2,18},{3,19},{4,20},{5,21},{6,22},{7,23},{8,24},{9,... | collective-permute-start | bytes 1572872 | tf_op jit(solution)/shard_map/ppermute | solution.py:41
  30.9 16.4 %collective-permute-start.19 = (bf16[512,1024]{1,0:T(8,128)(2,1)S(1)}, bf16[512,1024]{1,0:T(8,128)(2,1)S(1)}, u32[]{:S(2)}, u32[]{:S(2)}) collective-permute-start(bf16[512,1024]{1,0:T(8,128)(2,1)S(1)} %pad_maximum_fusion.refs_4_), channel_id=1, source_target_pairs={{0,4},{1,5},{2,6},{3,7},{4,0},{5,1},{6,2},{7,3},{8,12},{9,13},{10,... | collective-permute-start | bytes 3145736 | tf_op jit(solution)/shard_map/ppermute | solution.py:41
  33.1 6.9 %collective-permute-start.2 = (f32[1,3072]{1,0:T(1,128)S(1)}, f32[1,3072]{1,0:T(1,128)S(1)}, u32[]{:S(2)}, u32[]{:S(2)}) collective-permute-start(f32[1,3072]{1,0:T(1,128)S(1)} %broadcast_multiply_fusion), channel_id=1, source_target_pairs={{0,64},{1,65},{2,66},{3,67},{4,68},{5,69},{6,70},{7,71},{8,72},{9,... | collective-permute-start | bytes 36872 | tf_op jit(solution)/shard_map/ppermute | solution.py:355
  34.4 18.1 %collective-permute-start.20 = (bf16[512,1024]{1,0:T(8,128)(2,1)S(1)}, bf16[512,1024]{1,0:T(8,128)(2,1)S(1)}, u32[]{:S(2)}, u32[]{:S(2)}) collective-permute-start(bf16[512,1024]{1,0:T(8,128)(2,1)S(1)} %pad_maximum_fusion.refs_4_), channel_id=1, source_target_pairs={{0,12},{1,13},{2,14},{3,15},{4,8},{5,9},{6,10},{7,11},{8,4},{9,5},... | collective-permute-start | bytes 3145736 | tf_op jit(solution)/shard_map/ppermute | solution.py:41
  38.7 30.3 %collective-permute-start.3 = (bf16[2,2,128,1024]{3,2,1,0:T(8,128)(2,1)S(1)}, bf16[2,2,128,1024]{3,2,1,0:T(8,128)(2,1)S(1)}, u32[]{:S(2)}, u32[]{:S(2)}) collective-permute-start(bf16[2,2,128,1024]{3,2,1,0:T(8,128)(2,1)S(1)} %shard_map.142.own_ref), channel_id=1, source_target_pairs={{0,1},{1,2},{2,3},{3,0},{4,5},{5,6},{6,7},{7,4},{8,9},{9,10},{10,1... | collective-permute-start | bytes 3145736 | tf_op jit(solution)/shard_map/ppermute | solution.py:351
  40.0 31.0 %collective-permute-start.4 = (bf16[2,2,128,1024]{3,2,1,0:T(8,128)(2,1)S(1)}, bf16[2,2,128,1024]{3,2,1,0:T(8,128)(2,1)S(1)}, u32[]{:S(2)}, u32[]{:S(2)}) collective-permute-start(bf16[2,2,128,1024]{3,2,1,0:T(8,128)(2,1)S(1)} %shard_map.142.own_ref), channel_id=1, source_target_pairs={{0,3},{1,0},{2,1},{3,2},{4,7},{5,4},{6,5},{7,6},{8,11},{9,8},{10,9... | collective-permute-start | bytes 3145736 | tf_op jit(solution)/shard_map/ppermute | solution.py:351
  41.4 32.8 %collective-permute-start.5 = (bf16[2,2,128,1024]{3,2,1,0:T(8,128)(2,1)S(1)}, bf16[2,2,128,1024]{3,2,1,0:T(8,128)(2,1)S(1)}, u32[]{:S(2)}, u32[]{:S(2)}) collective-permute-start(bf16[2,2,128,1024]{3,2,1,0:T(8,128)(2,1)S(1)} %shard_map.142.own_ref), channel_id=1, source_target_pairs={{0,4},{1,5},{2,6},{3,7},{4,8},{5,9},{6,10},{7,11},{8,12},{9,13},{1... | collective-permute-start | bytes 3145736 | tf_op jit(solution)/shard_map/ppermute | solution.py:351
  41.5 33.9 %copy-start.15 = (f32[128]{0:T(128)S(1)}, f32[128]{0:T(128)}, u32[]{:S(2)}) copy-start(f32[128]{0:T(128)} %param.23) | copy-start | bytes 1540
  47.3 26.9 %copy-start.19 = (bf16[512,1024]{1,0:T(8,128)(2,1)}, bf16[512,1024]{1,0:T(8,128)(2,1)S(1)}, u32[]{:S(2)}) copy-start(bf16[512,1024]{1,0:T(8,128)(2,1)S(1)} %collective-permute-done.19.refs_5_) | copy-start | bytes 3145732
  47.3 9.7 %collective-permute-start.1 = (bf16[128,3072]{1,0:T(8,128)(2,1)S(1)}, bf16[128,3072]{1,0:T(8,128)(2,1)S(1)}, u32[]{:S(2)}, u32[]{:S(2)}) collective-permute-start(bf16[128,3072]{1,0:T(8,128)(2,1)S(1)} %multiply_convert_fusion), channel_id=1, source_target_pairs={{0,64},{1,65},{2,66},{3,67},{4,68},{5,69},{6,70},{7,71},{8,72},{9,... | collective-permute-start | bytes 2359304 | tf_op jit(solution)/shard_map/ppermute | solution.py:354
  52.6 22.8 %copy-start.20 = (bf16[512,1024]{1,0:T(8,128)(2,1)}, bf16[512,1024]{1,0:T(8,128)(2,1)S(1)}, u32[]{:S(2)}) copy-start(bf16[512,1024]{1,0:T(8,128)(2,1)S(1)} %collective-permute-done.20.refs_6_) | copy-start | bytes 3145732
  52.6 32.5 %collective-permute-start.6 = (bf16[2,2,128,1024]{3,2,1,0:T(8,128)(2,1)S(1)}, bf16[2,2,128,1024]{3,2,1,0:T(8,128)(2,1)}, u32[]{:S(2)}, u32[]{:S(2)}) collective-permute-start(bf16[2,2,128,1024]{3,2,1,0:T(8,128)(2,1)S(1)} %shard_map.142.own_ref), channel_id=1, source_target_pairs={{0,60},{1,61},{2,62},{3,63},{4,0},{5,1},{6,2},{7,3},{8,4},{9,5},{1... | collective-permute-start | bytes 3145736 | tf_op jit(solution)/shard_map/ppermute | solution.py:351
  57.9 30.5 %collective-permute-start.14 = (bf16[256,1024]{1,0:T(8,128)(2,1)}, bf16[256,1024]{1,0:T(8,128)(2,1)}, u32[]{:S(2)}, u32[]{:S(2)}) collective-permute-start(bf16[256,1024]{1,0:T(8,128)(2,1)} %pad_maximum_fusion.1.refs_0_), channel_id=1, source_target_pairs={{0,48},{1,49},{2,50},{3,51},{4,52},{5,53},{6,54},{7,55},{8,56},{9,... | collective-permute-start | bytes 1572872 | tf_op jit(solution)/shard_map/ppermute | solution.py:41
  69.9 18.5 %collective-permute-start.15 = (bf16[256,1024]{1,0:T(8,128)(2,1)}, bf16[256,1024]{1,0:T(8,128)(2,1)}, u32[]{:S(2)}, u32[]{:S(2)}) collective-permute-start(bf16[256,1024]{1,0:T(8,128)(2,1)} %collective-permute-done.13.refs_1_), channel_id=1, source_target_pairs={{0,48},{1,49},{2,50},{3,51},{4,52},{5,53},{6,54},{7,55},{8,56},{9,... | collective-permute-start | bytes 1572872 | tf_op jit(solution)/shard_map/ppermute | solution.py:41
  72.0 16.4 %collective-permute-start.21 = (bf16[256,1024]{1,0:T(8,128)(2,1)}, bf16[256,1024]{1,0:T(8,128)(2,1)}, u32[]{:S(2)}, u32[]{:S(2)}) collective-permute-start(bf16[256,1024]{1,0:T(8,128)(2,1)} %slice.16), channel_id=1, source_target_pairs={{0,12},{1,13},{2,14},{3,15},{4,8},{5,9},{6,10},{7,11},{8,4},{9,5},... | collective-permute-start | bytes 1572872 | tf_op jit(solution)/shard_map/ppermute | solution.py:41
  75.2 13.2 %collective-permute-start.22 = (bf16[256,1024]{1,0:T(8,128)(2,1)}, bf16[256,1024]{1,0:T(8,128)(2,1)}, u32[]{:S(2)}, u32[]{:S(2)}) collective-permute-start(bf16[256,1024]{1,0:T(8,128)(2,1)} %slice.17), channel_id=1, source_target_pairs={{0,4},{1,5},{2,6},{3,7},{4,0},{5,1},{6,2},{7,3},{8,12},{9,13},{10,... | collective-permute-start | bytes 1572872 | tf_op jit(solution)/shard_map/ppermute | solution.py:41
  93.8 6.1 %collective-permute-start.23 = (bf16[2,128,3072]{2,1,0:T(8,128)(2,1)S(1)}, bf16[2,128,3072]{2,1,0:T(8,128)(2,1)S(1)}, u32[]{:S(2)}, u32[]{:S(2)}) collective-permute-start(bf16[2,128,3072]{2,1,0:T(8,128)(2,1)S(1)} %shard_map.144.terms_ref), channel_id=1, source_target_pairs={{0,64},{64,0},{1,65},{65,1},{2,66},{66,2},{3,67},{67,3},{4,68},{68... | collective-permute-start | bytes 4718600 | tf_op jit(solution)/shard_map/ppermute | solution.py:361
  (18 other events, 93.7 us)
where the time goes:
time: 103 us; the launch traced here: 102 us
  starting transfers between devices  34.6 us (34%)
  waiting for transfers between devices  30.5 us (30%)
  Pallas kernels  19.1 us (19%)
  local copies, waits for them, and re-layouts  13.1 us (13%)
  other arithmetic  2.71 us (3%)
  between operations  2.54 us (2%)
    ppermute x16, starting transfers between devices, along(): return lax.ppermute(block, BOTH, pairs)  21.1 us
    ppermute x16, waiting for transfers between devices, along(): return lax.ppermute(block, BOTH, pairs)  16.3 us
    unnamed x52, local copies, waits for them, and re-layouts  11.4 us
    ppermute x4, waiting for transfers between devices, body(): around.append(lax.ppermute(pair, 'tile', neighbour_pairs(move)))  11.2 us
    pallas_call x2, Pallas kernels, project(): pl.pallas_call(make_project_kernel(gain.shape[-1], first, parts, normed_p...  5.97 us
    ppermute x4, starting transfers between devices, body(): around.append(lax.ppermute(pair, 'tile', neighbour_pairs(move)))  5.52 us
    pallas_call x1, Pallas kernels, output_project(): pl.pallas_call(make_output_kernel(shard), in_specs=[pl.BlockSpec(memory_s...  5.33 us
    pallas_call x1, Pallas kernels, attention(): pl.pallas_call(make_attend_kernel(head, factor), in_specs=[pl.BlockSpec(m...  3.2 us
  transfers between devices with their start and end apart: 24, of which 10 were waited for; matrix products, arithmetic and copies ran while one was open for 4% of the time, Pallas kernels for 11%

commit v1 on v0

--- a/solution.py
+++ b/solution.py
@@ -189,82 +189,141 @@
     return jnp.where(core == slot - 1, near, far)
 
 
-def make_output_kernel(shard):
-    def kernel(place_ref, a_ref, *refs):
-        pieces, out_ref, w_ref, sem = refs[:-3], refs[-3], refs[-2], refs[-1]
-        core = place_ref[0]
-        where = {"z": 1, "y": 2, "x": 3}
-        for colour, orders in enumerate(ORDERS):
-            unit = UNITS[colour]
-            parts = []
-            for level in range(3):
-                first, second = orders[0][level], orders[1][level]
-                place = jnp.where(core == 0, place_ref[where[first]], place_ref[where[second]])
-                stride = jnp.where(core == 0, STRIDES[first], STRIDES[second])
-                parts.append([slot_place(place, core, slot) * stride for slot in range(SIDE)])
-            mine = pieces[:SIDE] if colour == 0 else pieces[SIDE:]
-            blocks = [[(ref, at * unit) for at in range(SIDE * SIDE)] for ref in mine[: SIDE - 1]]
-            count = SIDE * SIDE // len(mine[SIDE - 1 :])
-            blocks.append([(ref, at * unit) for ref in mine[SIDE - 1 :] for at in range(count)])
-            for slot in range(SIDE):
-                for at, (ref, row) in enumerate(blocks[slot]):
-                    tile = parts[2][slot] + parts[1][at // SIDE] + parts[0][at % SIDE]
-                    target = pl.multiple_of(tile * shard + sum(UNITS[:colour]), 8)
-                    pltpu.make_async_copy(ref.at[pl.ds(row, unit)], w_ref.at[pl.ds(target, unit)], sem).start()
-        pltpu.make_async_copy(w_ref, w_ref, sem).wait()
-        steps, tokens, cols = a_ref.shape
-        left = a_ref[...].reshape(steps * tokens, cols)
-        chunk = 512
-        for at in range(0, w_ref.shape[0], chunk):
-            right = w_ref[at : at + chunk, :]
-            done = lax.dot_general(left, right, (((1,), (1,)), ((), ())), preferred_element_type=F32).astype(BF16)
-            for s in range(steps):
-                out_ref[1 - s, :, at : at + chunk] = done[s * tokens : (s + 1) * tokens]
-
-    return kernel
-
-
-def output_project(place, attended, pieces, width, shard):
+def placed_blocks(place_ref, shard, pieces, wanted):
+    core = place_ref[0]
+    where = {"z": 1, "y": 2, "x": 3}
+    found = []
+    for colour, orders in enumerate(ORDERS):
+        unit = UNITS[colour]
+        parts = []
+        for level in range(3):
+            first, second = orders[0][level], orders[1][level]
+            place = jnp.where(core == 0, place_ref[where[first]], place_ref[where[second]])
+            stride = jnp.where(core == 0, STRIDES[first], STRIDES[second])
+            parts.append([slot_place(place, core, slot) * stride for slot in range(SIDE)])
+        for slot in wanted:
+            refs = pieces[colour][slot - wanted[0]]
+            count = SIDE * SIDE // len(refs)
+            for at in range(SIDE * SIDE):
+                tile = parts[2][slot] + parts[1][at // SIDE] + parts[0][at % SIDE]
+                target = pl.multiple_of(tile * shard + sum(UNITS[:colour]), 8)
+                found.append((refs[at // count], at % count * unit, unit, target))
+    return found
+
+
+def start_placing(blocks, w_ref, sem):
+    for ref, row, rows, target in blocks:
+        pltpu.make_async_copy(ref.at[pl.ds(row, rows)], w_ref.at[pl.ds(target, rows)], sem).start()
+
+
+def in_hbm(values):
+    return [pltpu.with_memory_space_constraint(value, pltpu.HBM) for value in values]
+
+
+def place_early(place, pieces, width, shard):
+    flat = [piece for colour in pieces for piece in colour[: SIDE - 1]]
+    rows, cols = sum(piece.shape[0] for piece in flat), flat[0].shape[1]
+
+    def kernel(place_ref, *refs):
+        sources, w_ref, sem = refs[:-2], refs[-2], refs[-1]
+        by_colour = [[[ref] for ref in sources[: SIDE - 1]], [[ref] for ref in sources[SIDE - 1 :]]]
+        start_placing(placed_blocks(place_ref, shard, by_colour, range(SIDE - 1)), w_ref, sem)
+        pltpu.make_async_copy(w_ref.at[pl.ds(0, rows)], w_ref.at[pl.ds(0, rows)], sem).wait()
+
+    return pl.pallas_call(
+        kernel,
+        in_specs=[pl.BlockSpec(memory_space=pltpu.SMEM)] + [pl.BlockSpec(memory_space=pltpu.HBM)] * len(flat),
+        out_specs=pl.BlockSpec(memory_space=pltpu.VMEM),
+        out_shape=jax.ShapeDtypeStruct((width, cols), BF16),
+        scratch_shapes=[pltpu.SemaphoreType.DMA],
+        compiler_params=limit(2),
+        cost_estimate=pl.CostEstimate(flops=OUTPUT_COST // 4, transcendentals=0, bytes_accessed=4 * width * cols),
+    )(place, *in_hbm(flat))
+
+
+def multiply_into(a_ref, w_ref, out_ref, first):
+    steps, tokens, cols = a_ref.shape
+    left = a_ref[...].reshape(steps * tokens, cols)
+    chunk = 512
+    for at in range(0, out_ref.shape[2], chunk):
+        right = w_ref[first + at : first + at + chunk, :]
+        done = lax.dot_general(left, right, (((1,), (1,)), ((), ())), preferred_element_type=F32).astype(BF16)
+        for s in range(steps):
+            out_ref[1 - s, :, at : at + chunk] = done[s * tokens : (s + 1) * tokens]
+
+
+def output_first(place, attended, w, pieces, shard):
     steps, tokens, cols = attended.shape
-    return pl.pallas_call(
-        make_output_kernel(shard),
-        in_specs=[
-            pl.BlockSpec(memory_space=pltpu.SMEM),
-            pl.BlockSpec(memory_space=pltpu.VMEM),
-        ]
-        + [pl.BlockSpec(memory_space=pltpu.HBM)] * len(pieces),
+    width = w.shape[0]
+    flat = [piece for colour in pieces for piece in colour[SIDE - 1 :]]
+    counts = [len(colour) - SIDE + 1 for colour in pieces]
+    rows = sum(piece.shape[0] for piece in flat)
+
+    def kernel(place_ref, a_ref, w_in_ref, *refs):
+        sources, out_ref, w_ref, sem = refs[:-3], refs[-3], refs[-2], refs[-1]
+        by_colour = [[sources[: counts[0]]], [sources[counts[0] :]]]
+        start_placing(placed_blocks(place_ref, shard, by_colour, range(SIDE - 1, SIDE)), w_ref, sem)
+        pltpu.make_async_copy(w_ref.at[pl.ds(0, rows)], w_ref.at[pl.ds(0, rows)], sem).wait()
+        multiply_into(a_ref, w_ref, out_ref, 0)
+
+    return pl.pallas_call(
+        kernel,
+        in_specs=[pl.BlockSpec(memory_space=pltpu.SMEM)]
+        + [pl.BlockSpec(memory_space=pltpu.VMEM)] * 2
+        + [pl.BlockSpec(memory_space=pltpu.HBM)] * len(flat),
+        out_specs=[pl.BlockSpec(memory_space=pltpu.VMEM)] * 2,
+        out_shape=[
+            jax.ShapeDtypeStruct((steps, tokens, width // 2), BF16),
+            jax.ShapeDtypeStruct((width, cols), BF16),
+        ],
+        input_output_aliases={2: 1},
+        scratch_shapes=[pltpu.SemaphoreType.DMA],
+        compiler_params=limit(6),
+        cost_estimate=pl.CostEstimate(flops=OUTPUT_COST, transcendentals=0, bytes_accessed=2 * cols * width),
+    )(place, attended, w, *in_hbm(flat))
+
+
+def output_second(attended, w):
+    steps, tokens, cols = attended.shape
+    width = w.shape[0]
+
+    def kernel(a_ref, w_ref, out_ref):
+        multiply_into(a_ref, w_ref, out_ref, width // 2)
+
+    return pl.pallas_call(
+        kernel,
+        in_specs=[pl.BlockSpec(memory_space=pltpu.VMEM)] * 2,
         out_specs=pl.BlockSpec(memory_space=pltpu.VMEM),
-        out_shape=jax.ShapeDtypeStruct((steps, tokens, width), BF16),
-        scratch_shapes=[pltpu.VMEM((width, cols), BF16), pltpu.SemaphoreType.DMA],
-        compiler_params=limit(16),
+        out_shape=jax.ShapeDtypeStruct((steps, tokens, width // 2), BF16),
+        compiler_params=limit(6),
         cost_estimate=pl.CostEstimate(
-            flops=OUTPUT_COST,
-            transcendentals=0,
-            bytes_accessed=2 * (cols * width + steps * tokens * (cols + width)),
+            flops=steps * tokens * cols * width, transcendentals=0, bytes_accessed=cols * width
         ),
-    )(place, attended, *(pltpu.with_memory_space_constraint(piece, pltpu.HBM) for piece in pieces))
-
-
-def make_finish_kernel(parts):
+    )(attended, w)
+
+
+def make_finish_kernel(parts, first):
     def kernel(
-        place_ref, converged_ref, terms_ref, arrived_ref, start_ref, cached_ref, gate_ref, held_ref, pace_ref,
-        updated_ref, velocity_ref, buf_ref, sems,
+        place_ref, converged_ref, terms_ref, arrived_ref, start_ref, cached_ref, gate_ref, held_ref, pace_ref, *refs
     ):
+        updated_ref, velocity_ref, buf_ref, sems = refs[-4:]
         frozen = converged_ref[place_ref[0]] > 0
         frozen_first = converged_ref[0] > 0
-        gate = gate_ref[...]
-        pace = pace_ref[...]
-        rows = buf_ref.shape[2]
+        rows, cols = buf_ref.shape[2:]
+        span = slice(first, first + cols)
+        gate = gate_ref[:, span]
+        pace = pace_ref[:, span]
         copies = []
         for i in range(parts):
             at = slice(i * rows, (i + 1) * rows)
             mine = terms_ref[1, at, :].astype(F32) + arrived_ref[0, at, :].astype(F32)
-            buf_ref[i, 1] = jnp.where(frozen, cached_ref[at, :], gate * mine)
+            buf_ref[i, 1] = jnp.where(frozen, cached_ref[at, span], gate * mine)
             theirs = terms_ref[0, at, :].astype(F32) + arrived_ref[1, at, :].astype(F32)
-            prefix = jnp.where(frozen_first, held_ref[at, :].astype(F32), pace * theirs)
-            buf_ref[i, 0] = start_ref[at, :] + prefix
+            prefix = jnp.where(frozen_first, held_ref[at, span].astype(F32), pace * theirs)
+            buf_ref[i, 0] = start_ref[at, span] + prefix
             for j, ref in enumerate((updated_ref, velocity_ref)):
-                copy = pltpu.make_async_copy(buf_ref.at[i, j], ref.at[pl.ds(i * rows, rows)], sems.at[i, j])
+                target = ref.at[pl.ds(i * rows, rows), pl.ds(first, cols)]
+                copy = pltpu.make_async_copy(buf_ref.at[i, j], target, sems.at[i, j])
                 copy.start()
                 copies.append(copy)
         for copy in copies:
@@ -273,24 +332,27 @@
     return kernel
 
 
-def finish(place, converged, terms, arrived, start, cached, gate, held, pace):
+def finish(place, converged, terms, arrived, start, cached, gate, held, pace, first, so_far):
     tokens, width = start.shape
-    parts = 4
+    parts, cols = 4, terms.shape[2]
     out = jax.ShapeDtypeStruct((tokens, width), F32)
     return pl.pallas_call(
-        make_finish_kernel(parts),
-        in_specs=[pl.BlockSpec(memory_space=pltpu.SMEM)] * 2 + [pl.BlockSpec(memory_space=pltpu.VMEM)] * 7,
+        make_finish_kernel(parts, first),
+        in_specs=[pl.BlockSpec(memory_space=pltpu.SMEM)] * 2
+        + [pl.BlockSpec(memory_space=pltpu.VMEM)] * 7
+        + [pl.BlockSpec(memory_space=pltpu.HBM)] * len(so_far),
         out_specs=[pl.BlockSpec(memory_space=pltpu.HBM)] * 2,
         out_shape=[out, out],
+        input_output_aliases={9 + i: i for i in range(len(so_far))},
         scratch_shapes=[
-            pltpu.VMEM((parts, 2, tokens // parts, width), F32),
+            pltpu.VMEM((parts, 2, tokens // parts, cols), F32),
             pltpu.SemaphoreType.DMA((parts, 2)),
         ],
         compiler_params=limit(8),
         cost_estimate=pl.CostEstimate(
-            flops=8 * tokens * width, transcendentals=0, bytes_accessed=26 * tokens * width
+            flops=8 * tokens * cols, transcendentals=0, bytes_accessed=26 * tokens * cols
         ),
-    )(place, converged, terms, arrived, start, cached, gate, held, pace)
+    )(place, converged, terms, arrived, start, cached, gate, held, pace, *so_far)
 
 
 def start_gather(w_out):
@@ -343,7 +405,7 @@
     other = lax.ppermute(own, "step", SWAP)
 
     lines = start_gather(w_out)
-    pieces = finish_gather("a", lines[0]) + finish_gather("b", lines[1])
+    pieces = [finish_gather("a", lines[0]), finish_gather("b", lines[1])]
 
     pair = project(own, other, w_qkv, k_gain[None], 1, 2, 1)
     around = []
@@ -356,12 +418,14 @@
     queries = project(own, other, w_qkv, q_gain[None], 0, 1, 1)
     queries, sent_cached, sent_gate = lax.optimization_barrier((queries, sent_cached, sent_gate))
     attended = attention(neighbours, queries, [pair] + around, head)
-    terms = output_project(place, attended, pieces, width, shard)
-
-    arrived = lax.ppermute(terms, "step", SWAP)
-    updated, velocity = finish(
-        place, converged[:, 0], terms, arrived, start, cached_velocity[0], gate, sent_cached, sent_gate
-    )
+    w_placed = place_early(place, pieces, width, shard)
+    left, w_placed = output_first(place, attended, w_placed, pieces, shard)
+    left_arrived = lax.ppermute(left, "step", SWAP)
+    right = output_second(attended, w_placed)
+    right_arrived = lax.ppermute(right, "step", SWAP)
+    rest = (start, cached_velocity[0], gate, sent_cached, sent_gate)
+    outs = finish(place, converged[:, 0], left, left_arrived, *rest, 0, ())
+    updated, velocity = finish(place, converged[:, 0], right, right_arrived, *rest, width // 2, tuple(outs))
     return (updated[None], velocity[None])
 
 

time: 103 us -> 108 us (1.049)
  waiting for transfers between devices: 30.5 us -> 35.1 us
  Pallas kernels: 19.1 us -> 22.3 us
  other arithmetic: 2.71 us -> 1.09 us
  starting transfers between devices: 34.6 us -> 33.1 us
    ppermute x4, waiting for transfers between devices: 11.2 us -> 18.2 us  [body(): around.append(lax.ppermute(pair, 'tile', neighbour_pairs(move)))]
    ppermute x16, starting transfers between devices: 21.1 us -> 17.2 us  [along(): return lax.ppermute(block, BOTH, pairs)]
    pallas_call x2 -> x5, Pallas kernels: 7.77 us -> 10.7 us  [the longest x2 3.67 us: finish(): pl.pallas_call(make_finish_kernel(parts, first), in_specs=[pl.BlockSpec(m...]
    ppermute x1 -> x2, waiting for transfers between devices: 3.04 us -> 0.76 us  [the longest x1 0.76 us: body(): left_arrived = lax.ppermute(left, 'step', SWAP)]
    ppermute x1 -> x2, starting transfers between devices: 3.07 us -> 4.8 us  [the longest x1 4.67 us: body(): left_arrived = lax.ppermute(left, 'step', SWAP)]
    concatenate x3, other arithmetic: 1.75 us -> 0.13 us  [four(): jnp.concatenate([block, first, second, along(block, dims, 0, opposite)],...]
    unnamed x52 -> x54, local copies, waits for them, and re-layouts: 11.4 us -> 11.2 us
  transfers between devices with their start and end apart: 24 -> 25, of which waited for: 10 -> 9; matrix products, arithmetic and copies ran while one was open for 4% -> 2% of each run, Pallas kernels for 11% -> 16%
where the time goes in v1:
time: 108 us; the launch traced here: 107 us
  waiting for transfers between devices  35.1 us (32%)
  starting transfers between devices  33.1 us (31%)
  Pallas kernels  22.3 us (21%)
  local copies, waits for them, and re-layouts  13 us (12%)
  between operations  2.65 us (2%)
  other arithmetic  1.09 us (1%)
    ppermute x4, waiting for transfers between devices, body(): around.append(lax.ppermute(pair, 'tile', neighbour_pairs(move)))  18.2 us
    ppermute x16, starting transfers between devices, along(): return lax.ppermute(block, BOTH, pairs)  17.2 us
    ppermute x16, waiting for transfers between devices, along(): return lax.ppermute(block, BOTH, pairs)  16.1 us
    unnamed x54, local copies, waits for them, and re-layouts  11.2 us
    ppermute x4, starting transfers between devices, body(): around.append(lax.ppermute(pair, 'tile', neighbour_pairs(move)))  6.24 us
    pallas_call x2, Pallas kernels, project(): pl.pallas_call(make_project_kernel(gain.shape[-1], first, parts, normed_p...  5.97 us
    ppermute x1, starting transfers between devices, body(): left_arrived = lax.ppermute(left, 'step', SWAP)  4.67 us
    pallas_call x2, Pallas kernels, finish(): pl.pallas_call(make_finish_kernel(parts, first), in_specs=[pl.BlockSpec(m...  3.67 us
  transfers between devices with their start and end apart: 25, of which 9 were waited for; matrix products, arithmetic and copies ran while one was open for 2% of the time, Pallas kernels for 16%

profile of v1, /device:TPU:1, one launch (start us, length us, event | category | flops | bytes accessed | tf_op | source)
XLA Modules:
  0.0 107.2 jit_solution(10258091903861907899)
XLA Ops:
  0.6 3.8 %collective-permute-start.9 = (bf16[1,48,1024]{2,1,0:T(8,128)(2,1)}, bf16[1,48,1024]{2,1,0:T(8,128)(2,1)S(1)}, u32[]{:S(2)}, u32[]{:S(2)}) collective-permute-start(bf16[1,48,1024]{2,1,0:T(8,128)(2,1)} %bitcast.38), channel_id=1, source_target_pairs={{0,2},{1,3},{2,0},{3,1},{4,6},{5,7},{6,4},{7,5},{8,10},{9,11},{10,... | collective-permute-start | bytes 294920 | tf_op jit(solution)/shard_map/ppermute | solution.py:41
  5.2 1.4 %collective-permute-done.9 = bf16[1,48,1024]{2,1,0:T(8,128)(2,1)S(1)} collective-permute-done((bf16[1,48,1024]{2,1,0:T(8,128)(2,1)}, bf16[1,48,1024]{2,1,0:T(8,128)(2,1)S(1)}, u32[]{:S(2)}, u32[]{:S(2)}) %collective-permute-start.9) | collective-permute-done | bytes 98336 | tf_op jit(solution)/shard_map/ppermute | solution.py:41
  6.7 1.5 %collective-permute-done.8 = bf16[1,48,1024]{2,1,0:T(8,128)(2,1)S(1)} collective-permute-done((bf16[1,48,1024]{2,1,0:T(8,128)(2,1)}, bf16[1,48,1024]{2,1,0:T(8,128)(2,1)S(1)}, u32[]{:S(2)}, u32[]{:S(2)}) %collective-permute-start.8) | collective-permute-done | bytes 98336 | tf_op jit(solution)/shard_map/ppermute | solution.py:41
  8.1 1.9 %collective-permute-done.7 = bf16[1,48,1024]{2,1,0:T(8,128)(2,1)S(1)} collective-permute-done((bf16[1,48,1024]{2,1,0:T(8,128)(2,1)}, bf16[1,48,1024]{2,1,0:T(8,128)(2,1)S(1)}, u32[]{:S(2)}, u32[]{:S(2)}) %collective-permute-start.7) | collective-permute-done | bytes 98336 | tf_op jit(solution)/shard_map/ppermute | solution.py:41
  10.8 2.5 %collective-permute-start.12 = (bf16[64,1024]{1,0:T(8,128)(2,1)S(1)}, bf16[64,1024]{1,0:T(8,128)(2,1)S(1)}, u32[]{:S(2)}, u32[]{:S(2)}) collective-permute-start(bf16[64,1024]{1,0:T(8,128)(2,1)S(1)} %bitcast.34), channel_id=1, source_target_pairs={{0,8},{1,9},{2,10},{3,11},{4,12},{5,13},{6,14},{7,15},{8,0},{9,1},... | collective-permute-start | bytes 393224 | tf_op jit(solution)/shard_map/ppermute | solution.py:41
  14.2 2.1 %shard_map.140.own_ref = bf16[128,3072]{1,0:T(8,128)(2,1)S(1)} custom-call(f32[128,3072]{1,0:T(8,128)} %bitcast.43, f32[1,3072]{1,0:T(1,128)} %scale_any.1, f32[1,3072]{1,0:T(1,128)} %shift_any.1), custom_call_target="tpu_custom_call" | custom-call | flops 16000000000 | bytes 2359296 | tf_op jit(solution)/shard_map/pallas_call | solution.py:78
  16.4 2.3 %collective-permute-start = (bf16[128,3072]{1,0:T(8,128)(2,1)S(1)}, bf16[128,3072]{1,0:T(8,128)(2,1)S(1)}, u32[]{:S(2)}, u32[]{:S(2)}) collective-permute-start(bf16[128,3072]{1,0:T(8,128)(2,1)S(1)} %shard_map.140.own_ref), channel_id=1, source_target_pairs={{0,64},{64,0},{1,65},{65,1},{2,66},{66,2},{3,67},{67,3},{4,68},{68... | collective-permute-start | bytes 2359304 | tf_op jit(solution)/shard_map/ppermute | solution.py:405
  20.1 3.7 %collective-permute-start.17 = (bf16[128,1024]{1,0:T(8,128)(2,1)S(1)}, bf16[128,1024]{1,0:T(8,128)(2,1)S(1)}, u32[]{:S(2)}, u32[]{:S(2)}) collective-permute-start(bf16[128,1024]{1,0:T(8,128)(2,1)S(1)} %bitcast.30), channel_id=1, source_target_pairs={{0,32},{1,33},{2,34},{3,35},{4,36},{5,37},{6,38},{7,39},{8,40},{9,... | collective-permute-start | bytes 786440 | tf_op jit(solution)/shard_map/ppermute | solution.py:41
  25.4 5.1 %collective-permute-done.17 = bf16[128,1024]{1,0:T(8,128)(2,1)S(1)} collective-permute-done((bf16[128,1024]{1,0:T(8,128)(2,1)S(1)}, bf16[128,1024]{1,0:T(8,128)(2,1)S(1)}, u32[]{:S(2)}, u32[]{:S(2)}) %collective-permute-start.17) | collective-permute-done | bytes 262176 | tf_op jit(solution)/shard_map/ppermute | solution.py:41
  30.6 1.3 %collective-permute-start.2 = (f32[1,3072]{1,0:T(1,128)S(1)}, f32[1,3072]{1,0:T(1,128)S(1)}, u32[]{:S(2)}, u32[]{:S(2)}) collective-permute-start(f32[1,3072]{1,0:T(1,128)S(1)} %broadcast_multiply_fusion), channel_id=1, source_target_pairs={{0,64},{1,65},{2,66},{3,67},{4,68},{5,69},{6,70},{7,71},{8,72},{9,... | collective-permute-start | bytes 36872 | tf_op jit(solution)/shard_map/ppermute | solution.py:417
  31.8 4.8 %collective-permute-done.16 = bf16[128,1024]{1,0:T(8,128)(2,1)S(1)} collective-permute-done((bf16[128,1024]{1,0:T(8,128)(2,1)S(1)}, bf16[128,1024]{1,0:T(8,128)(2,1)S(1)}, u32[]{:S(2)}, u32[]{:S(2)}) %collective-permute-start.16) | collective-permute-done | bytes 262176 | tf_op jit(solution)/shard_map/ppermute | solution.py:41
  36.8 1.8 %collective-permute-start.18 = (bf16[512,1024]{1,0:T(8,128)(2,1)S(1)}, bf16[512,1024]{1,0:T(8,128)(2,1)S(1)}, u32[]{:S(2)}, u32[]{:S(2)}) collective-permute-start(bf16[512,1024]{1,0:T(8,128)(2,1)S(1)} %pad_maximum_fusion.refs_3_), channel_id=1, source_target_pairs={{0,4},{1,5},{2,6},{3,7},{4,0},{5,1},{6,2},{7,3},{8,12},{9,13},{10,... | collective-permute-start | bytes 3145736 | tf_op jit(solution)/shard_map/ppermute | solution.py:41
  38.7 3.8 %shard_map.142.own_ref = bf16[2,2,128,1024]{3,2,1,0:T(8,128)(2,1)S(1)} custom-call(bf16[128,3072]{1,0:T(8,128)(2,1)S(1)} %shard_map.140.own_ref, bf16[128,3072]{1,0:T(8,128)(2,1)S(1)} %collective-permute-done.other_ref, bf16[3,3072,1024]{2,1,0:T(8,128)(2,1)S(1)} %bitcast.21, f32[1,128]{1,0:T(1,128)S(1)} %bitcast.26), custom_call_target="tpu_custom_call" | custom-call | flops 3221225472 | bytes 14155776 | tf_op jit(solution)/shard_map/pallas_call | solution.py:121
  42.6 4.5 %collective-permute-start.6 = (bf16[2,2,128,1024]{3,2,1,0:T(8,128)(2,1)S(1)}, bf16[2,2,128,1024]{3,2,1,0:T(8,128)(2,1)S(1)}, u32[]{:S(2)}, u32[]{:S(2)}) collective-permute-start(bf16[2,2,128,1024]{3,2,1,0:T(8,128)(2,1)S(1)} %shard_map.142.own_ref), channel_id=1, source_target_pairs={{0,60},{1,61},{2,62},{3,63},{4,0},{5,1},{6,2},{7,3},{8,4},{9,5},{1... | collective-permute-start | bytes 3145736 | tf_op jit(solution)/shard_map/ppermute | solution.py:413
  48.0 1.3 %collective-permute-start.1 = (bf16[128,3072]{1,0:T(8,128)(2,1)S(1)}, bf16[128,3072]{1,0:T(8,128)(2,1)S(1)}, u32[]{:S(2)}, u32[]{:S(2)}) collective-permute-start(bf16[128,3072]{1,0:T(8,128)(2,1)S(1)} %multiply_convert_fusion), channel_id=1, source_target_pairs={{0,64},{1,65},{2,66},{3,67},{4,68},{5,69},{6,70},{7,71},{8,72},{9,... | collective-permute-start | bytes 2359304 | tf_op jit(solution)/shard_map/ppermute | solution.py:416
  49.3 1.4 %collective-permute-done.19.refs_5_ = bf16[512,1024]{1,0:T(8,128)(2,1)S(1)} collective-permute-done((bf16[512,1024]{1,0:T(8,128)(2,1)S(1)}, bf16[512,1024]{1,0:T(8,128)(2,1)S(1)}, u32[]{:S(2)}, u32[]{:S(2)}) %collective-permute-start.19) | collective-permute-done | bytes 1048608 | tf_op jit(solution)/shard_map/ppermute | solution.py:41
  50.7 1.7 %collective-permute-start.4 = (bf16[2,2,128,1024]{3,2,1,0:T(8,128)(2,1)S(1)}, bf16[2,2,128,1024]{3,2,1,0:T(8,128)(2,1)}, u32[]{:S(2)}, u32[]{:S(2)}) collective-permute-start(bf16[2,2,128,1024]{3,2,1,0:T(8,128)(2,1)S(1)} %shard_map.142.own_ref), channel_id=1, source_target_pairs={{0,3},{1,0},{2,1},{3,2},{4,7},{5,4},{6,5},{7,6},{8,11},{9,8},{10,9... | collective-permute-start | bytes 3145736 | tf_op jit(solution)/shard_map/ppermute | solution.py:413
  52.5 0.9 slice.17
  55.9 14.1 %collective-permute-done.6.d_ref = bf16[2,2,128,1024]{3,2,1,0:T(8,128)(2,1)S(1)} collective-permute-done((bf16[2,2,128,1024]{3,2,1,0:T(8,128)(2,1)S(1)}, bf16[2,2,128,1024]{3,2,1,0:T(8,128)(2,1)S(1)}, u32[]{:S(2)}, u32[]{:S(2)}) %collective-permute-start.6) | collective-permute-done | bytes 1048608 | tf_op jit(solution)/shard_map/ppermute | solution.py:413
  70.1 1.0 copy-done.7
  71.6 4.0 %collective-permute-done.5.c_ref = bf16[2,2,128,1024]{3,2,1,0:T(8,128)(2,1)S(1)} collective-permute-done((bf16[2,2,128,1024]{3,2,1,0:T(8,128)(2,1)S(1)}, bf16[2,2,128,1024]{3,2,1,0:T(8,128)(2,1)S(1)}, u32[]{:S(2)}, u32[]{:S(2)}) %collective-permute-start.5) | collective-permute-done | bytes 1048608 | tf_op jit(solution)/shard_map/ppermute | solution.py:413
  75.6 1.0 copy-done.9
  77.4 6.4 %copy-done = bf16[3,3072,1024]{2,1,0:T(8,128)(2,1)S(1)} copy-done((bf16[3,3072,1024]{2,1,0:T(8,128)(2,1)S(1)}, bf16[3,3072,1024]{2,1,0:T(8,128)(2,1)}, u32[]{:S(2)}) %copy-start) | copy-done | bytes 18874392
  83.8 1.1 %copy-done.4 = bf16[128,3072]{1,0:T(8,128)(2,1)S(1)} copy-done((bf16[128,3072]{1,0:T(8,128)(2,1)S(1)}, bf16[128,3072]{1,0:T(8,128)(2,1)}, u32[]{:S(2)}) %copy-start.4) | copy-done | bytes 786456
  84.9 2.1 %shard_map.141.q_ref = bf16[1,2,128,1024]{3,2,1,0:T(8,128)(2,1)S(1)} custom-call(bf16[128,3072]{1,0:T(8,128)(2,1)S(1)} %shard_map.140.own_ref, bf16[128,3072]{1,0:T(8,128)(2,1)S(1)} %copy-done.4, bf16[3,3072,1024]{2,1,0:T(8,128)(2,1)S(1)} %copy-done, f32[1,128]{1,0:T(1,128)S(1)} %bitcast.27), custom_call_target="tpu_custom_call" | custom-call | flops 1610612736 | bytes 7864320 | tf_op jit(solution)/shard_map/pallas_call | solution.py:121
  87.1 3.0 %shard_map.144.w_in_ref = bf16[3072,1024]{1,0:T(8,128)(2,1)S(1)} custom-call(s32[4]{0:T(128)S(1)} %pad_add_fusion.place_ref, bf16[256,1024]{1,0:T(8,128)(2,1)} %copy-done.19, bf16[256,1024]{1,0:T(8,128)(2,1)} %collective-permute-done.13.refs_1_, bf16[256,1024]{1,0:T(8,128)(2,1)} %copy-done.20, bf16[512,1024]{1,0:T(8,128)(2,1)} %copy-done.16, ...), custom_call_target="tpu_custom_call" | custom-call | flops 2000000000 | bytes 12582912 | tf_op jit(solution)/shard_map/pallas_call | solution.py:233
  90.2 3.5 %shard_map.143.a_ref = bf16[2,128,1024]{2,1,0:T(8,128)(2,1)S(1)} custom-call(s32[1,4]{1,0:T(1,128)S(1)} %copy-done.15, bf16[1,2,128,1024]{3,2,1,0:T(8,128)(2,1)S(1)} %shard_map.141.q_ref, bf16[2,2,128,1024]{3,2,1,0:T(8,128)(2,1)S(1)} %shard_map.142.own_ref, bf16[2,2,128,1024]{3,2,1,0:T(8,128)(2,1)} %collective-permute-done.3.a_ref, ...), custom_call_target="tpu_custom_call" | custom-call | flops 671088640 | bytes 6291456 | tf_op jit(solution)/shard_map/pallas_call | solution.py:167
  93.7 3.0 %shard_map.145 = (bf16[2,128,1536]{2,1,0:T(8,128)(2,1)S(1)}, bf16[3072,1024]{1,0:T(8,128)(2,1)S(1)}) custom-call(s32[4]{0:T(128)S(1)} %pad_add_fusion.place_ref, bf16[2,128,1024]{2,1,0:T(8,128)(2,1)S(1)} %shard_map.143.a_ref, bf16[3072,1024]{1,0:T(8,128)(2,1)S(1)} %shard_map.144.w_in_ref, ...), custom_call_target="tpu_custom_call", output_to_operand_aliasing={{1}: (2, {})} | custom-call | flops 8000000000 | bytes 6291456 | tf_op jit(solution)/shard_map/pallas_call | solution.py:269
  96.7 4.7 %collective-permute-start.24 = (bf16[2,128,1536]{2,1,0:T(8,128)(2,1)S(1)}, bf16[2,128,1536]{2,1,0:T(8,128)(2,1)S(1)}, u32[]{:S(2)}, u32[]{:S(2)}) collective-permute-start(bf16[2,128,1536]{2,1,0:T(8,128)(2,1)S(1)} %get-tuple-element.15.terms_ref), channel_id=1, source_target_pairs={{0,64},{64,0},{1,65},{65,1},{2,66},{66,2},{3,67},{67,3},{4,68},{68... | collective-permute-start | bytes 2359304 | tf_op jit(solution)/shard_map/ppermute | solution.py:423
  101.4 1.0 shard_map.146.terms_ref
  103.3 1.8 %shard_map.147 = (f32[128,3072]{1,0:T(8,128)}, f32[128,3072]{1,0:T(8,128)}) custom-call(s32[4]{0:T(128)S(1)} %pad_add_fusion.place_ref, s32[2]{0:T(128)S(1)} %bitcast.24, bf16[2,128,1536]{2,1,0:T(8,128)(2,1)S(1)} %get-tuple-element.15.terms_ref, bf16[2,128,1536]{2,1,0:T(8,128)(2,1)S(1)} %collective-permute-done.24.arrived_ref, f32[128,3072]{1,0:T(8,128)S(1)} %copy-done.2, ...), custom_call_target="tpu_custom_call" | custom-call | flops 1572864 | bytes 5111808 | tf_op jit(solution)/shard_map/pallas_call | solution.py:339
  105.2 1.8 %shard_map.148 = (f32[128,3072]{1,0:T(8,128)}, f32[128,3072]{1,0:T(8,128)}) custom-call(s32[4]{0:T(128)S(1)} %pad_add_fusion.place_ref, s32[2]{0:T(128)S(1)} %bitcast.25, bf16[2,128,1536]{2,1,0:T(8,128)(2,1)S(1)} %shard_map.146.terms_ref, ...), custom_call_target="tpu_custom_call", output_to_operand_aliasing={{0}: (9, {}), {1}: (10, {})} | custom-call | flops 1572864 | bytes 5111808 | tf_op jit(solution)/shard_map/pallas_call | solution.py:339
  (91 shorter events, 10.0 us)
Async XLA Ops:
  0.6 6.0 %collective-permute-start.9 = (bf16[1,48,1024]{2,1,0:T(8,128)(2,1)}, bf16[1,48,1024]{2,1,0:T(8,128)(2,1)S(1)}, u32[]{:S(2)}, u32[]{:S(2)}) collective-permute-start(bf16[1,48,1024]{2,1,0:T(8,128)(2,1)} %bitcast.38), channel_id=1, source_target_pairs={{0,2},{1,3},{2,0},{3,1},{4,6},{5,7},{6,4},{7,5},{8,10},{9,11},{10,... | collective-permute-start | bytes 294920 | tf_op jit(solution)/shard_map/ppermute | solution.py:41
  4.4 3.7 %collective-permute-start.8 = (bf16[1,48,1024]{2,1,0:T(8,128)(2,1)}, bf16[1,48,1024]{2,1,0:T(8,128)(2,1)S(1)}, u32[]{:S(2)}, u32[]{:S(2)}) collective-permute-start(bf16[1,48,1024]{2,1,0:T(8,128)(2,1)} %bitcast.39), channel_id=1, source_target_pairs={{0,3},{1,2},{2,1},{3,0},{4,7},{5,6},{6,5},{7,4},{8,11},{9,10},{10,... | collective-permute-start | bytes 294920 | tf_op jit(solution)/shard_map/ppermute | solution.py:41
  4.8 5.2 %collective-permute-start.7 = (bf16[1,48,1024]{2,1,0:T(8,128)(2,1)}, bf16[1,48,1024]{2,1,0:T(8,128)(2,1)S(1)}, u32[]{:S(2)}, u32[]{:S(2)}) collective-permute-start(bf16[1,48,1024]{2,1,0:T(8,128)(2,1)} %bitcast.40), channel_id=1, source_target_pairs={{0,1},{1,0},{2,3},{3,2},{4,5},{5,4},{6,7},{7,6},{8,9},{9,8},{10,11... | collective-permute-start | bytes 294920 | tf_op jit(solution)/shard_map/ppermute | solution.py:41
  10.8 13.0 %collective-permute-start.12 = (bf16[64,1024]{1,0:T(8,128)(2,1)S(1)}, bf16[64,1024]{1,0:T(8,128)(2,1)S(1)}, u32[]{:S(2)}, u32[]{:S(2)}) collective-permute-start(bf16[64,1024]{1,0:T(8,128)(2,1)S(1)} %bitcast.34), channel_id=1, source_target_pairs={{0,8},{1,9},{2,10},{3,11},{4,12},{5,13},{6,14},{7,15},{8,0},{9,1},... | collective-permute-start | bytes 393224 | tf_op jit(solution)/shard_map/ppermute | solution.py:41
  13.3 11.2 %collective-permute-start.11 = (bf16[64,1024]{1,0:T(8,128)(2,1)S(1)}, bf16[64,1024]{1,0:T(8,128)(2,1)S(1)}, u32[]{:S(2)}, u32[]{:S(2)}) collective-permute-start(bf16[64,1024]{1,0:T(8,128)(2,1)S(1)} %bitcast.35), channel_id=1, source_target_pairs={{0,12},{1,13},{2,14},{3,15},{4,8},{5,9},{6,10},{7,11},{8,4},{9,5},... | collective-permute-start | bytes 393224 | tf_op jit(solution)/shard_map/ppermute | solution.py:41
  13.6 10.9 %collective-permute-start.10 = (bf16[64,1024]{1,0:T(8,128)(2,1)S(1)}, bf16[64,1024]{1,0:T(8,128)(2,1)S(1)}, u32[]{:S(2)}, u32[]{:S(2)}) collective-permute-start(bf16[64,1024]{1,0:T(8,128)(2,1)S(1)} %bitcast.36), channel_id=1, source_target_pairs={{0,4},{1,5},{2,6},{3,7},{4,0},{5,1},{6,2},{7,3},{8,12},{9,13},{10,... | collective-permute-start | bytes 393224 | tf_op jit(solution)/shard_map/ppermute | solution.py:41
  14.2 24.5 %slice-start = ((s8[18874368]{0:T(1024)(128)(4,1)}), s8[4194304]{0:T(1024)(128)(4,1)S(1)}, s32[]{:S(2)}) async-start(s8[18874368]{0:T(1024)(128)(4,1)} %bitcast.20), calls=%async_computation | async-start | bytes 8388608
  14.2 24.5 %slice-start.1 = ((s8[18874368]{0:T(1024)(128)(4,1)}), s8[4194304]{0:T(1024)(128)(4,1)S(1)}, s32[]{:S(2)}) async-start(s8[18874368]{0:T(1024)(128)(4,1)} %bitcast.20), calls=%async_computation.1 | async-start | bytes 8388608
  14.2 24.5 %slice-start.2 = ((s8[18874368]{0:T(1024)(128)(4,1)}), s8[4194304]{0:T(1024)(128)(4,1)S(1)}, s32[]{:S(2)}) async-start(s8[18874368]{0:T(1024)(128)(4,1)} %bitcast.20), calls=%async_computation.2 | async-start | bytes 8388608
  14.2 24.4 %slice-start.3 = ((s8[18874368]{0:T(1024)(128)(4,1)}), s8[4194304]{0:T(1024)(128)(4,1)S(1)}, s32[]{:S(2)}) async-start(s8[18874368]{0:T(1024)(128)(4,1)} %bitcast.20), calls=%async_computation.3 | async-start | bytes 8388608
  16.4 20.4 %collective-permute-start = (bf16[128,3072]{1,0:T(8,128)(2,1)S(1)}, bf16[128,3072]{1,0:T(8,128)(2,1)S(1)}, u32[]{:S(2)}, u32[]{:S(2)}) collective-permute-start(bf16[128,3072]{1,0:T(8,128)(2,1)S(1)} %shard_map.140.own_ref), channel_id=1, source_target_pairs={{0,64},{64,0},{1,65},{65,1},{2,66},{66,2},{3,67},{67,3},{4,68},{68... | collective-permute-start | bytes 2359304 | tf_op jit(solution)/shard_map/ppermute | solution.py:405
  20.1 10.4 %collective-permute-start.17 = (bf16[128,1024]{1,0:T(8,128)(2,1)S(1)}, bf16[128,1024]{1,0:T(8,128)(2,1)S(1)}, u32[]{:S(2)}, u32[]{:S(2)}) collective-permute-start(bf16[128,1024]{1,0:T(8,128)(2,1)S(1)} %bitcast.30), channel_id=1, source_target_pairs={{0,32},{1,33},{2,34},{3,35},{4,36},{5,37},{6,38},{7,39},{8,40},{9,... | collective-permute-start | bytes 786440 | tf_op jit(solution)/shard_map/ppermute | solution.py:41
  23.8 12.8 %collective-permute-start.16 = (bf16[128,1024]{1,0:T(8,128)(2,1)S(1)}, bf16[128,1024]{1,0:T(8,128)(2,1)S(1)}, u32[]{:S(2)}, u32[]{:S(2)}) collective-permute-start(bf16[128,1024]{1,0:T(8,128)(2,1)S(1)} %bitcast.31), channel_id=1, source_target_pairs={{0,48},{1,49},{2,50},{3,51},{4,52},{5,53},{6,54},{7,55},{8,56},{9,... | collective-permute-start | bytes 786440 | tf_op jit(solution)/shard_map/ppermute | solution.py:41
  24.6 12.1 %collective-permute-start.15 = (bf16[128,1024]{1,0:T(8,128)(2,1)S(1)}, bf16[128,1024]{1,0:T(8,128)(2,1)S(1)}, u32[]{:S(2)}, u32[]{:S(2)}) collective-permute-start(bf16[128,1024]{1,0:T(8,128)(2,1)S(1)} %bitcast.32), channel_id=1, source_target_pairs={{0,16},{1,17},{2,18},{3,19},{4,20},{5,21},{6,22},{7,23},{8,24},{9,... | collective-permute-start | bytes 786440 | tf_op jit(solution)/shard_map/ppermute | solution.py:41
  24.6 22.5 %collective-permute-start.14 = (bf16[256,1024]{1,0:T(8,128)(2,1)S(1)}, bf16[256,1024]{1,0:T(8,128)(2,1)S(1)}, u32[]{:S(2)}, u32[]{:S(2)}) collective-permute-start(bf16[256,1024]{1,0:T(8,128)(2,1)S(1)} %pad_maximum_fusion.1.refs_0_), channel_id=1, source_target_pairs={{0,48},{1,49},{2,50},{3,51},{4,52},{5,53},{6,54},{7,55},{8,56},{9,... | collective-permute-start | bytes 1572872 | tf_op jit(solution)/shard_map/ppermute | solution.py:41
  30.6 12.0 %collective-permute-start.2 = (f32[1,3072]{1,0:T(1,128)S(1)}, f32[1,3072]{1,0:T(1,128)S(1)}, u32[]{:S(2)}, u32[]{:S(2)}) collective-permute-start(f32[1,3072]{1,0:T(1,128)S(1)} %broadcast_multiply_fusion), channel_id=1, source_target_pairs={{0,64},{1,65},{2,66},{3,67},{4,68},{5,69},{6,70},{7,71},{8,72},{9,... | collective-permute-start | bytes 36872 | tf_op jit(solution)/shard_map/ppermute | solution.py:417
  36.6 11.4 %collective-permute-start.13 = (bf16[256,1024]{1,0:T(8,128)(2,1)S(1)}, bf16[256,1024]{1,0:T(8,128)(2,1)}, u32[]{:S(2)}, u32[]{:S(2)}) collective-permute-start(bf16[256,1024]{1,0:T(8,128)(2,1)S(1)} %pad_maximum_fusion.1.refs_0_), channel_id=1, source_target_pairs={{0,16},{1,17},{2,18},{3,19},{4,20},{5,21},{6,22},{7,23},{8,24},{9,... | collective-permute-start | bytes 1572872 | tf_op jit(solution)/shard_map/ppermute | solution.py:41
  36.7 14.0 %collective-permute-start.19 = (bf16[512,1024]{1,0:T(8,128)(2,1)S(1)}, bf16[512,1024]{1,0:T(8,128)(2,1)S(1)}, u32[]{:S(2)}, u32[]{:S(2)}) collective-permute-start(bf16[512,1024]{1,0:T(8,128)(2,1)S(1)} %pad_maximum_fusion.refs_3_), channel_id=1, source_target_pairs={{0,12},{1,13},{2,14},{3,15},{4,8},{5,9},{6,10},{7,11},{8,4},{9,5},... | collective-permute-start | bytes 3145736 | tf_op jit(solution)/shard_map/ppermute | solution.py:41
  36.8 15.6 %collective-permute-start.18 = (bf16[512,1024]{1,0:T(8,128)(2,1)S(1)}, bf16[512,1024]{1,0:T(8,128)(2,1)S(1)}, u32[]{:S(2)}, u32[]{:S(2)}) collective-permute-start(bf16[512,1024]{1,0:T(8,128)(2,1)S(1)} %pad_maximum_fusion.refs_3_), channel_id=1, source_target_pairs={{0,4},{1,5},{2,6},{3,7},{4,0},{5,1},{6,2},{7,3},{8,12},{9,13},{10,... | collective-permute-start | bytes 3145736 | tf_op jit(solution)/shard_map/ppermute | solution.py:41
  42.6 27.5 %collective-permute-start.6 = (bf16[2,2,128,1024]{3,2,1,0:T(8,128)(2,1)S(1)}, bf16[2,2,128,1024]{3,2,1,0:T(8,128)(2,1)S(1)}, u32[]{:S(2)}, u32[]{:S(2)}) collective-permute-start(bf16[2,2,128,1024]{3,2,1,0:T(8,128)(2,1)S(1)} %shard_map.142.own_ref), channel_id=1, source_target_pairs={{0,60},{1,61},{2,62},{3,63},{4,0},{5,1},{6,2},{7,3},{8,4},{9,5},{1... | collective-permute-start | bytes 3145736 | tf_op jit(solution)/shard_map/ppermute | solution.py:413
  47.1 28.5 %collective-permute-start.5 = (bf16[2,2,128,1024]{3,2,1,0:T(8,128)(2,1)S(1)}, bf16[2,2,128,1024]{3,2,1,0:T(8,128)(2,1)S(1)}, u32[]{:S(2)}, u32[]{:S(2)}) collective-permute-start(bf16[2,2,128,1024]{3,2,1,0:T(8,128)(2,1)S(1)} %shard_map.142.own_ref), channel_id=1, source_target_pairs={{0,4},{1,5},{2,6},{3,7},{4,8},{5,9},{6,10},{7,11},{8,12},{9,13},{1... | collective-permute-start | bytes 3145736 | tf_op jit(solution)/shard_map/ppermute | solution.py:413
  47.9 29.6 %copy-start.14 = (f32[128]{0:T(128)S(1)}, f32[128]{0:T(128)}, u32[]{:S(2)}) copy-start(f32[128]{0:T(128)} %param.23) | copy-start | bytes 1540
  48.0 6.3 %collective-permute-start.1 = (bf16[128,3072]{1,0:T(8,128)(2,1)S(1)}, bf16[128,3072]{1,0:T(8,128)(2,1)S(1)}, u32[]{:S(2)}, u32[]{:S(2)}) collective-permute-start(bf16[128,3072]{1,0:T(8,128)(2,1)S(1)} %multiply_convert_fusion), channel_id=1, source_target_pairs={{0,64},{1,65},{2,66},{3,67},{4,68},{5,69},{6,70},{7,71},{8,72},{9,... | collective-permute-start | bytes 2359304 | tf_op jit(solution)/shard_map/ppermute | solution.py:416
  50.7 24.9 %copy-start.17 = (bf16[512,1024]{1,0:T(8,128)(2,1)}, bf16[512,1024]{1,0:T(8,128)(2,1)S(1)}, u32[]{:S(2)}) copy-start(bf16[512,1024]{1,0:T(8,128)(2,1)S(1)} %collective-permute-done.19.refs_5_) | copy-start | bytes 3145732
  50.7 39.4 %collective-permute-start.4 = (bf16[2,2,128,1024]{3,2,1,0:T(8,128)(2,1)S(1)}, bf16[2,2,128,1024]{3,2,1,0:T(8,128)(2,1)}, u32[]{:S(2)}, u32[]{:S(2)}) collective-permute-start(bf16[2,2,128,1024]{3,2,1,0:T(8,128)(2,1)S(1)} %shard_map.142.own_ref), channel_id=1, source_target_pairs={{0,3},{1,0},{2,1},{3,2},{4,7},{5,4},{6,5},{7,6},{8,11},{9,8},{10,9... | collective-permute-start | bytes 3145736 | tf_op jit(solution)/shard_map/ppermute | solution.py:413
  52.5 24.9 %copy-start.18 = (bf16[512,1024]{1,0:T(8,128)(2,1)}, bf16[512,1024]{1,0:T(8,128)(2,1)S(1)}, u32[]{:S(2)}) copy-start(bf16[512,1024]{1,0:T(8,128)(2,1)S(1)} %collective-permute-done.18.refs_4_) | copy-start | bytes 3145732
  52.5 37.7 %collective-permute-start.3 = (bf16[2,2,128,1024]{3,2,1,0:T(8,128)(2,1)S(1)}, bf16[2,2,128,1024]{3,2,1,0:T(8,128)(2,1)}, u32[]{:S(2)}, u32[]{:S(2)}) collective-permute-start(bf16[2,2,128,1024]{3,2,1,0:T(8,128)(2,1)S(1)} %shard_map.142.own_ref), channel_id=1, source_target_pairs={{0,1},{1,2},{2,3},{3,0},{4,5},{5,6},{6,7},{7,4},{8,9},{9,10},{10,1... | collective-permute-start | bytes 3145736 | tf_op jit(solution)/shard_map/ppermute | solution.py:413
  55.2 38.5 %collective-permute-start.20 = (bf16[256,1024]{1,0:T(8,128)(2,1)}, bf16[256,1024]{1,0:T(8,128)(2,1)}, u32[]{:S(2)}, u32[]{:S(2)}) collective-permute-start(bf16[256,1024]{1,0:T(8,128)(2,1)} %collective-permute-done.13.refs_1_), channel_id=1, source_target_pairs={{0,48},{1,49},{2,50},{3,51},{4,52},{5,53},{6,54},{7,55},{8,56},{9,... | collective-permute-start | bytes 1572872 | tf_op jit(solution)/shard_map/ppermute | solution.py:41
  71.0 22.7 %collective-permute-start.22 = (bf16[256,1024]{1,0:T(8,128)(2,1)}, bf16[256,1024]{1,0:T(8,128)(2,1)}, u32[]{:S(2)}, u32[]{:S(2)}) collective-permute-start(bf16[256,1024]{1,0:T(8,128)(2,1)} %slice.17), channel_id=1, source_target_pairs={{0,4},{1,5},{2,6},{3,7},{4,0},{5,1},{6,2},{7,3},{8,12},{9,13},{10,... | collective-permute-start | bytes 1572872 | tf_op jit(solution)/shard_map/ppermute | solution.py:41
  76.6 17.1 %collective-permute-start.21 = (bf16[256,1024]{1,0:T(8,128)(2,1)}, bf16[256,1024]{1,0:T(8,128)(2,1)}, u32[]{:S(2)}, u32[]{:S(2)}) collective-permute-start(bf16[256,1024]{1,0:T(8,128)(2,1)} %slice.16), channel_id=1, source_target_pairs={{0,12},{1,13},{2,14},{3,15},{4,8},{5,9},{6,10},{7,11},{8,4},{9,5},... | collective-permute-start | bytes 1572872 | tf_op jit(solution)/shard_map/ppermute | solution.py:41
  96.7 6.6 %collective-permute-start.24 = (bf16[2,128,1536]{2,1,0:T(8,128)(2,1)S(1)}, bf16[2,128,1536]{2,1,0:T(8,128)(2,1)S(1)}, u32[]{:S(2)}, u32[]{:S(2)}) collective-permute-start(bf16[2,128,1536]{2,1,0:T(8,128)(2,1)S(1)} %get-tuple-element.15.terms_ref), channel_id=1, source_target_pairs={{0,64},{64,0},{1,65},{65,1},{2,66},{66,2},{3,67},{67,3},{4,68},{68... | collective-permute-start | bytes 2359304 | tf_op jit(solution)/shard_map/ppermute | solution.py:423
  102.4 2.7 %collective-permute-start.23 = (bf16[2,128,1536]{2,1,0:T(8,128)(2,1)S(1)}, bf16[2,128,1536]{2,1,0:T(8,128)(2,1)S(1)}, u32[]{:S(2)}, u32[]{:S(2)}) collective-permute-start(bf16[2,128,1536]{2,1,0:T(8,128)(2,1)S(1)} %shard_map.146.terms_ref), channel_id=1, source_target_pairs={{0,64},{64,0},{1,65},{65,1},{2,66},{66,2},{3,67},{67,3},{4,68},{68... | collective-permute-start | bytes 2359304 | tf_op jit(solution)/shard_map/ppermute | solution.py:425
  (20 other events, 128.7 us)
